TPU v7x, 32 devices: a 4x4x1 block of a 4x4x8 slice. The times are simulated.
32 devices in a mesh: dp: 1 (over z), pool: 4 (over y), ep: 8 (over x, core).
Axes of the slice: x: 4, y: 4, z: 1, core: 2. Of those that a mesh axis runs over, the one named last changes fastest.
The devices are a block of a 4x4x8 slice.
Arguments:
- x: bfloat16 [2048, 1536], P(('dp', 'ep', 'pool'))
- k_cache: bfloat16 [2, 2048, 128, 2, 128], P(None, ('dp', 'ep'))
- v_cache: bfloat16 [2, 2048, 128, 2, 128], P(None, ('dp', 'ep'))
- cache_len: int32 [2048], P(('dp', 'ep'))
- w_query: bfloat16 [2, 1536, 1536], replicated
- w_key: bfloat16 [2, 1536, 256], replicated
- w_value: bfloat16 [2, 1536, 256], replicated
- w_out: bfloat16 [2, 1536, 1536], replicated
- w_router: float32 [2, 1536, 8], replicated
- expert_ids: int32 [2, 2048, 2], P(None, ('dp', 'ep'))
- w_gate: bfloat16 [2, 8, 1536, 4096], P(None, 'ep')
- w_up: bfloat16 [2, 8, 1536, 4096], P(None, 'ep')
- w_down: bfloat16 [2, 8, 4096, 1536], P(None, 'ep')
- shared_gate: bfloat16 [2, 1536, 4096], replicated
- shared_up: bfloat16 [2, 1536, 4096], replicated
- shared_down: bfloat16 [2, 4096, 1536], replicated
Outputs:
- output: bfloat16 [2048, 1536], P(('dp', 'ep', 'pool'))
All inputs are finite; a program needn't handle non-finite values.
Results may differ from a plain program's by a relative error of at most 0.0184699.
Values are sent between devices in bfloat16 or wider.
A program may use at most 768 MiB of HBM per device.

v0:
```python
import math
import functools
import jax
import jax.numpy as jnp
from jax import lax
from jax.sharding import PartitionSpec as P

RMS_EPS = 1e-6
ROPE_BASE = 10000.0


def rms_norm(vals):
    flt = vals.astype(jnp.float32)
    return flt * lax.rsqrt(jnp.mean(flt * flt, axis=-1, keepdims=True) + RMS_EPS)


def rotate(vals, pos):
    half = vals.shape[-1] // 2
    inv_freq = jnp.exp(jnp.arange(half, dtype=jnp.float32) * (-math.log(ROPE_BASE) / half))
    angle = pos.astype(jnp.float32)[:, None, None] * inv_freq
    cosine = jnp.cos(angle)
    sine = jnp.sin(angle)
    first = vals[..., :half]
    second = vals[..., half:]
    return jnp.concatenate([first * cosine - second * sine, second * cosine + first * sine], axis=-1)


def attention_block(state, lens, k_layer, v_layer, w_query, w_key, w_value, w_out, q_heads, kv_heads):
    n_tok = state.shape[0]
    head_dim = k_layer.shape[-1]
    hidden = rms_norm(state).astype(jnp.bfloat16)
    query = jnp.dot(hidden, w_query, preferred_element_type=jnp.float32).reshape(n_tok, q_heads, head_dim)
    key_new = jnp.dot(hidden, w_key, preferred_element_type=jnp.float32).reshape(n_tok, kv_heads, head_dim)
    val_new = jnp.dot(hidden, w_value, preferred_element_type=jnp.float32).astype(jnp.bfloat16).reshape(n_tok, kv_heads, head_dim)
    query = rotate(query, lens).astype(jnp.bfloat16).reshape(n_tok, kv_heads, q_heads // kv_heads, head_dim)
    key_new = rotate(key_new, lens).astype(jnp.bfloat16)
    scale = head_dim ** -0.5
    s_cache = jnp.einsum("nkgd,nskd->nkgs", query, k_layer, preferred_element_type=jnp.float32) * scale
    s_new = jnp.einsum("nkgd,nkd->nkg", query, key_new, preferred_element_type=jnp.float32) * scale
    valid = jnp.arange(k_layer.shape[1])[None, None, None, :] < lens[:, None, None, None]
    s_cache = jnp.where(valid, s_cache, -jnp.inf)
    peak_val = jnp.maximum(jnp.max(s_cache, axis=-1), s_new)
    e_cache = jnp.exp(s_cache - peak_val[..., None])
    e_new = jnp.exp(s_new - peak_val)
    total_exp = jnp.sum(e_cache, axis=-1) + e_new
    p_cache = (e_cache / total_exp[..., None]).astype(jnp.bfloat16)
    p_new = (e_new / total_exp).astype(jnp.bfloat16)
    mixed = jnp.einsum("nkgs,nskd->nkgd", p_cache, v_layer, preferred_element_type=jnp.float32)
    mixed = mixed + p_new.astype(jnp.float32)[..., None] * val_new.astype(jnp.float32)[:, :, None, :]
    attn = mixed.astype(jnp.bfloat16).reshape(n_tok, q_heads * head_dim)
    resid = (state.astype(jnp.float32) + jnp.dot(attn, w_out, preferred_element_type=jnp.float32)).astype(jnp.bfloat16)
    return resid, rms_norm(resid).astype(jnp.bfloat16)


def router_gates(normed, w_router, choice_ids):
    logits = jnp.dot(normed.astype(jnp.float32), w_router)
    return jax.nn.softmax(jnp.take_along_axis(logits, choice_ids, axis=1), axis=-1)


def gated_mlp(normed, w_gate, w_up, w_down):
    mid = (jax.nn.silu(jnp.dot(normed, w_gate, preferred_element_type=jnp.float32)) * jnp.dot(normed, w_up, preferred_element_type=jnp.float32)).astype(jnp.bfloat16)
    return jnp.dot(mid, w_down, preferred_element_type=jnp.float32).astype(jnp.bfloat16)


def expert_rows(rows, locs, exp_local, w_gate, w_up, w_down):
    order = jnp.argsort(locs, stable=True)
    inverse = jnp.argsort(order, stable=True)
    sorted_rows = jnp.take(rows, order, axis=0)
    sizes = jnp.bincount(locs, length=exp_local + 1)[:exp_local].astype(jnp.int32)
    gate_part = lax.ragged_dot(sorted_rows, w_gate, sizes, preferred_element_type=jnp.float32)
    up_part = lax.ragged_dot(sorted_rows, w_up, sizes, preferred_element_type=jnp.float32)
    mid = (jax.nn.silu(gate_part) * up_part).astype(jnp.bfloat16)
    out_sorted = lax.ragged_dot(mid, w_down, sizes, preferred_element_type=jnp.float32).astype(jnp.bfloat16)
    return jnp.take(out_sorted, inverse, axis=0)


def combine_out(resid, normed, gates, pair_out, shared_gate, shared_up, shared_down):
    routed = jnp.sum(gates[..., None] * pair_out.astype(jnp.float32), axis=1)
    shared_out = gated_mlp(normed, shared_gate, shared_up, shared_down)
    return (resid.astype(jnp.float32) + routed + shared_out.astype(jnp.float32)).astype(jnp.bfloat16)


def solution(mesh):
    pool_size = mesh.shape["pool"]
    ep_size = mesh.shape["ep"]
    half_pool = pool_size // 2
    to_att = [(half_pool + idx, idx) for idx in range(half_pool)]
    to_exp = [(idx, half_pool + idx) for idx in range(half_pool)]
    row_spec = P(("dp", "ep", "pool"), None)
    cache_spec = P(None, ("dp", "ep"), None, None, None)
    expert_spec = P(None, "ep", None, None)
    in_specs = (row_spec, cache_spec, cache_spec, P(("dp", "ep")), P(), P(), P(), P(), P(), P(None, ("dp", "ep"), None), expert_spec, expert_spec, expert_spec, P(), P(), P())

    def body(x_loc, k_cache, v_cache, cache_len, w_query, w_key, w_value, w_out, w_router, expert_ids, w_gate, w_up, w_down, shared_gate, shared_up, shared_down):
        tok_dev, d_model = x_loc.shape
        head_dim = k_cache.shape[4]
        kv_heads = k_cache.shape[3]
        q_heads = w_query.shape[2] // head_dim
        top_k = expert_ids.shape[2]
        exp_local = w_gate.shape[1]
        group_tok = 2 * tok_dev
        capacity = 3 * tok_dev * top_k // ep_size
        slots = ep_size * capacity
        pool_idx = lax.axis_index("pool")
        is_att = pool_idx < half_pool
        sub_idx = pool_idx % half_pool

        def my_rows(arr, axis):
            arr_shape = arr.shape
            split = arr.reshape(arr_shape[:axis] + (2, half_pool, tok_dev) + arr_shape[axis + 1:])
            picked = lax.dynamic_index_in_dim(split, sub_idx, axis=axis + 1, keepdims=False)
            return picked.reshape(arr_shape[:axis] + (group_tok,) + arr_shape[axis + 1:])

        my_len = my_rows(cache_len, 0)
        my_ids = my_rows(expert_ids, 1)

        def attention_stage(x_cur, layer):
            resid, normed = attention_block(x_cur, my_len, my_rows(k_cache[layer], 0), my_rows(v_cache[layer], 0), w_query[layer], w_key[layer], w_value[layer], w_out[layer], q_heads, kv_heads)
            choice_ids = my_ids[layer]
            gates = router_gates(normed, w_router[layer], choice_ids)
            flat_ids = choice_ids.reshape(-1)
            dest_dev = flat_ids // exp_local
            onehot = (dest_dev[:, None] == jnp.arange(ep_size)[None, :]).astype(jnp.int32)
            pair_rank = jnp.sum(jnp.cumsum(onehot, axis=0) * onehot, axis=1) - 1
            slot_of = dest_dev * capacity + pair_rank
            src_tok = jnp.zeros((slots,), jnp.int32).at[slot_of].set(jnp.arange(group_tok * top_k, dtype=jnp.int32) // top_k)
            send_loc = jnp.full((slots,), exp_local, jnp.int32).at[slot_of].set(flat_ids % exp_local)
            return resid, normed, gates, slot_of, jnp.take(normed, src_tok, axis=0), send_loc

        def skip_attention(x_cur):
            blank = jnp.zeros((group_tok, d_model), jnp.bfloat16)
            return (blank, blank, jnp.zeros((group_tok, top_k), jnp.float32), jnp.zeros((group_tok * top_k,), jnp.int32), jnp.zeros((slots, d_model), jnp.bfloat16), jnp.full((slots,), exp_local, jnp.int32))

        def expert_stage(rows, locs, layer):
            return expert_rows(rows, locs, exp_local, w_gate[layer], w_up[layer], w_down[layer])

        def skip_experts(rows, locs):
            return jnp.zeros_like(rows)

        def combine_stage(resid, normed, gates, slot_of, returned, layer):
            pair_out = jnp.take(returned, slot_of, axis=0).reshape(group_tok, top_k, d_model)
            return combine_out(resid, normed, gates, pair_out, shared_gate[layer], shared_up[layer], shared_down[layer])

        def skip_combine(resid, normed, gates, slot_of, returned):
            return jnp.zeros_like(resid)

        x_in = lax.ppermute(x_loc, "pool", to_att)
        x_att = jnp.concatenate([x_loc, x_in], axis=0)
        for layer in range(k_cache.shape[0]):
            resid, normed, gates, slot_of, send_rows, send_loc = lax.cond(is_att, functools.partial(attention_stage, layer=layer), skip_attention, x_att)
            recv_rows = lax.ppermute(lax.all_to_all(send_rows, "ep", 0, 0, tiled=True), "pool", to_exp)
            recv_loc = lax.ppermute(lax.all_to_all(send_loc, "ep", 0, 0, tiled=True), "pool", to_exp)
            expert_out = lax.cond(is_att, skip_experts, functools.partial(expert_stage, layer=layer), recv_rows, recv_loc)
            returned = lax.all_to_all(lax.ppermute(expert_out, "pool", to_att), "ep", 0, 0, tiled=True)
            x_att = lax.cond(is_att, functools.partial(combine_stage, layer=layer), skip_combine, resid, normed, gates, slot_of, returned)
        x_back = lax.ppermute(x_att[tok_dev:], "pool", to_exp)
        return jnp.where(is_att, x_att[:tok_dev], x_back)

    return jax.shard_map(body, mesh=mesh, in_specs=in_specs, out_specs=row_spec, check_vma=False)
```

profile of v0, /device:TPU:97, one launch (start us, length us, event | category | flops | bytes accessed | tf_op | source)
XLA Modules:
  0.0 709.0 jit_solution(7027199771709335355)
XLA Ops:
  4.2 6.1 collective-permute-done
  11.3 126.6 %conditional.6 = (bf16[128,1536]{1,0:T(8,128)(2,1)}, bf16[128,1536]{1,0:T(8,128)(2,1)}, f32[128,2]{1,0:T(8,128)S(1)}, s32[256]{0:T(256)S(1)}, bf16[384,1536]{1,0:T(8,128)(2,1)}, /*index=5*/s32[384]{0:T(512)S(1)}) conditional(s32[]{:T(128)} %convert_element_type.170, () %tuple.52, (bf16[128,1536]{1,0:T(8,128)(2,1)S(1)}, s32[2,64]{1,0:T(2,128)S(1)}, ...), branch_computations={%region_0.1_spmd, %region_1.15_spmd} | conditional | flops 1523576704 | bytes 300678144 | solution.py:150
  11.3 14.1 %slice.95 = bf16[1,256,128,2,128]{4,3,2,1,0:T(2,128)(2,1)} slice(bf16[2,256,128,2,128]{4,3,2,1,0:T(2,128)(2,1)} %get-tuple-element.130), slice={[0:1], [0:256], [0:128], [0:2], [0:128]} | slice | bytes 33554432 | tf_op jit(solution)/shard_map/cond/branch_1_fun/slice | solution.py:118
  25.4 14.3 %slice.91 = bf16[1,256,128,2,128]{4,3,2,1,0:T(2,128)(2,1)} slice(bf16[2,256,128,2,128]{4,3,2,1,0:T(2,128)(2,1)} %get-tuple-element.126), slice={[0:1], [0:256], [0:128], [0:2], [0:128]} | slice | bytes 33554432 | tf_op jit(solution)/shard_map/cond/branch_1_fun/slice | solution.py:118
  39.7 2.2 copy-done
  41.9 16.5 %constant_dynamic-slice_fusion = (bf16[2,1,64,128,2,128]{5,4,3,2,1,0:T(2,128)(2,1)}, bf16[2,1,64,128,2,128]{5,4,3,2,1,0:T(2,128)(2,1)}) fusion(bf16[2,2,64,128,2,128]{5,4,3,2,1,0:T(2,128)(2,1)S(1)} %bitcast.220, s32[]{:T(128)S(6)} %select_n.92, bf16[2,2,64,128,2,128]{5,4,3,2,1,0:T(2,128)(2,1)} %bitcast.222), kind=kLoop, calls=%fused_computation.164 | loop fusion | bytes 33554436 | tf_op jit(solution)/shard_map/cond/branch_1_fun/jit(dynamic_index_in_dim)/dynamic_slice | solution.py:111
  58.4 9.2 %copy.125 = bf16[2,1,64,128,2,128]{5,3,4,2,0,1:T(8,128)(2,1)} copy(bf16[2,1,64,128,2,128]{5,4,3,2,1,0:T(2,128)(2,1)} %get-tuple-element.367) | data formatting | bytes 16777216 | tf_op jit(solution)/shard_map/cond
  67.7 9.2 %copy.124 = bf16[2,1,64,128,2,128]{5,3,4,2,0,1:T(8,128)(2,1)} copy(bf16[2,1,64,128,2,128]{5,4,3,2,1,0:T(2,128)(2,1)} %get-tuple-element.368) | data formatting | bytes 16777216 | tf_op jit(solution)/shard_map/cond
  76.9 12.7 %copy.106 = bf16[2,1536,1536]{1,2,0:T(8,128)(2,1)} copy(bf16[2,1536,1536]{2,1,0:T(8,128)(2,1)} %get-tuple-element.323) | data formatting | bytes 18874368 | tf_op jit(solution)/shard_map
  89.8 2.2 slice-done
  91.9 1.5 fusion.87
  94.8 9.1 %fusion.151 = (f32[128,2,6]{2,1,0:T(2,128)S(1)}, f32[128,2,6,128]{3,2,1,0:T(8,128)}) fusion(bf16[128,128,2,128]{3,1,2,0:T(8,128)(2,1)} %bitcast.224, bf16[128,2,6,64]{3,2,1,0:T(8,128)(2,1)S(1)} %copy.86, bf16[128,2,6,64]{3,2,1,0:T(8,128)(2,1)S(1)} %copy.85, pred[128,128]{1,0:T(8,128)(4,1)S(1)} %iota_compare_fusion), kind=kOutput, calls=%fused_computation.259 | convolution fusion | flops 51706368 | bytes 9590784 | tf_op jit(solution)/shard_map/cond/branch_1_fun/nkgd,nskd->nkgs/dot_general | solution.py:38
  106.0 2.0 copy.107
  112.2 5.7 fusion.74
  118.3 3.9 fusion.77
  122.3 1.9 fusion.78
  125.5 1.4 gather_fusion.6
  128.9 1.4 scatter_custom_fusion
  130.3 4.7 gather_fusion.7
  136.3 1.4 scatter_custom_fusion.1
  137.8 22.8 %all_to_all.70 = bf16[8,48,1536]{2,1,0:T(8,128)(2,1)S(1)} all-to-all(bf16[8,48,1536]{2,1,0:T(8,128)(2,1)} %bitcast.65), channel_id=1, replica_groups=mesh['dp'=1,'pool'=4,'ep'=8] {'ep'}, dimensions={0} | all-to-all | bytes 2359296 | tf_op jit(solution)/shard_map/all_to_all | solution.py:151
  162.1 7.9 %all_to_all.71 = s32[8,48,1]{1,2,0:T(1,128)S(1)} all-to-all(s32[8,48,1]{1,2,0:T(1,128)S(1)} %bitcast.242), channel_id=1, replica_groups=mesh['dp'=1,'pool'=4,'ep'=8] {'ep'}, dimensions={0} | all-to-all | bytes 3072 | tf_op jit(solution)/shard_map/all_to_all | solution.py:152
  172.0 14.7 %collective-permute-done.1 = s32[384]{0:T(512)S(1)} collective-permute-done((s32[384]{0:T(512)S(1)}, s32[384]{0:T(512)S(1)}, u32[]{:S(2)}, u32[]{:S(2)}) %collective-permute-start.1) | collective-permute-done | bytes 1568 | tf_op jit(solution)/shard_map/ppermute | solution.py:152
  188.1 122.6 %collective-permute-done.3 = bf16[384,1536]{1,0:T(8,128)(2,1)} collective-permute-done((bf16[384,1536]{1,0:T(8,128)(2,1)S(1)}, bf16[384,1536]{1,0:T(8,128)(2,1)}, u32[]{:S(2)}, u32[]{:S(2)}) %collective-permute-start.3) | collective-permute-done | bytes 1179680 | tf_op jit(solution)/shard_map/ppermute | solution.py:154
  310.7 6.9 all-to-all-start.2
  317.6 16.2 %all-to-all-done.2 = bf16[8,48,1536]{2,1,0:T(8,128)(2,1)S(1)} async-done(((bf16[8,48,1536]{2,1,0:T(8,128)(2,1)}), bf16[8,48,1536]{2,1,0:T(8,128)(2,1)S(1)}, u32[]{:S(2)}, u32[]{:S(2)}) %all-to-all-start.2) | async-done | bytes 1179680 | tf_op jit(solution)/shard_map/all_to_all | solution.py:154
  333.8 30.3 %conditional.8 = (bf16[128,1536]{1,0:T(8,128)(2,1)S(1)}) conditional(s32[]{:T(128)} %convert_element_type.170, () %tuple.51, (bf16[128,1536]{1,0:T(8,128)(2,1)}, f32[128,2]{1,0:T(8,128)S(1)}, bf16[8,48,1536]{2,1,0:T(8,128)(2,1)S(1)}, s32[256]{0:T(256)S(1)}, bf16[2,1536,4096]{2,1,0:T(8,128)(2,1)}, /*index=5*/bf16[128,1536]{1,0:T(8,128)(2,1)}, ...), branch_computations={%region_18.22_spmd, %region_19.25_spmd} | conditional | flops 4837542912 | bytes 53750280 | solution.py:155
  333.8 2.2 gather_fusion.4
  336.0 2.5 select_convert_fusion
  338.4 3.0 reshape.433
  341.5 3.6 multiply_reduce_fusion
  345.1 7.9 %fusion.6 = f32[128,4096]{1,0:T(8,128)} fusion(bf16[128,1536]{1,0:T(8,128)(2,1)} %get-tuple-element.146, bf16[2,1536,4096]{2,1,0:T(8,128)(2,1)} %get-tuple-element.147), kind=kOutput, calls=%fused_computation.35 | convolution fusion | flops 1610612736 | bytes 15073280 | tf_op jit(solution)/shard_map/cond/branch_1_fun/dot_general | solution.py:61
  353.0 11.1 %fusion.26 = bf16[128,1536]{1,0:T(8,128)(2,1)S(1)} fusion(bf16[2,4096,1536]{2,1,0:T(8,128)(2,1)} %get-tuple-element.149, f32[128,1536]{1,0:T(8,128)S(1)} %multiply_reduce_fusion, bf16[128,1536]{1,0:T(8,128)(2,1)} %get-tuple-element.142, bf16[128,1536]{1,0:T(8,128)(2,1)} %get-tuple-element.146, bf16[2,1536,4096]{2,1,0:T(8,128)(2,1)} %get-tuple-element.148, ...), kind=kOutput, calls=%fused_computation.45 | convolution fusion | flops 3225550848 | bytes 29229056 | tf_op jit(solution)/shard_map/cond/branch_1_fun/dot_general | solution.py:62
  364.1 127.3 %conditional.9 = (bf16[128,1536]{1,0:T(8,128)(2,1)}, bf16[128,1536]{1,0:T(8,128)(2,1)}, f32[128,2]{1,0:T(8,128)}, s32[256]{0:T(256)S(1)}, bf16[384,1536]{1,0:T(8,128)(2,1)}, /*index=5*/s32[384]{0:T(512)S(1)}) conditional(s32[]{:T(128)} %convert_element_type.170, () %tuple.50, (bf16[128,1536]{1,0:T(8,128)(2,1)S(1)}, s32[2,64]{1,0:T(2,128)S(1)}, ...), branch_computations={%region_21.26_spmd, %region_22.38_spmd} | conditional | flops 1523576704 | bytes 294390784 | solution.py:150
  364.5 14.1 %slice.116 = bf16[1,256,128,2,128]{4,3,2,1,0:T(2,128)(2,1)} slice(bf16[2,256,128,2,128]{4,3,2,1,0:T(2,128)(2,1)} %get-tuple-element.157), slice={[1:2], [0:256], [0:128], [0:2], [0:128]} | slice | bytes 33554432 | tf_op jit(solution)/shard_map/cond/branch_1_fun/slice | solution.py:118
  378.7 14.3 %slice.112 = bf16[1,256,128,2,128]{4,3,2,1,0:T(2,128)(2,1)} slice(bf16[2,256,128,2,128]{4,3,2,1,0:T(2,128)(2,1)} %get-tuple-element.154), slice={[1:2], [0:256], [0:128], [0:2], [0:128]} | slice | bytes 33554432 | tf_op jit(solution)/shard_map/cond/branch_1_fun/slice | solution.py:118
  393.0 2.2 copy-done.1
  395.2 16.5 %constant_dynamic-slice_fusion.2 = (bf16[2,1,64,128,2,128]{5,4,3,2,1,0:T(2,128)(2,1)}, bf16[2,1,64,128,2,128]{5,4,3,2,1,0:T(2,128)(2,1)}) fusion(bf16[2,2,64,128,2,128]{5,4,3,2,1,0:T(2,128)(2,1)S(1)} %bitcast.221, s32[]{:T(128)S(6)} %select_n.100, bf16[2,2,64,128,2,128]{5,4,3,2,1,0:T(2,128)(2,1)} %bitcast.223), kind=kLoop, calls=%fused_computation.247 | loop fusion | bytes 33554436 | tf_op jit(solution)/shard_map/cond/branch_1_fun/jit(dynamic_index_in_dim)/dynamic_slice | solution.py:111
  411.7 9.2 %copy.128 = bf16[2,1,64,128,2,128]{5,3,4,2,0,1:T(8,128)(2,1)} copy(bf16[2,1,64,128,2,128]{5,4,3,2,1,0:T(2,128)(2,1)} %get-tuple-element.385) | data formatting | bytes 16777216 | tf_op jit(solution)/shard_map/cond
  420.9 9.2 %copy.127 = bf16[2,1,64,128,2,128]{5,3,4,2,0,1:T(8,128)(2,1)} copy(bf16[2,1,64,128,2,128]{5,4,3,2,1,0:T(2,128)(2,1)} %get-tuple-element.386) | data formatting | bytes 16777216 | tf_op jit(solution)/shard_map/cond
  430.1 12.7 %copy.109 = bf16[2,1536,1536]{1,2,0:T(8,128)(2,1)} copy(bf16[2,1536,1536]{2,1,0:T(8,128)(2,1)} %get-tuple-element.335) | data formatting | bytes 18874368 | tf_op jit(solution)/shard_map
  443.0 2.2 slice-done.1
  445.2 1.5 fusion.130
  448.1 9.0 %fusion.152 = (f32[128,2,6]{2,1,0:T(2,128)S(1)}, f32[128,2,6,128]{3,2,1,0:T(8,128)}) fusion(bf16[128,128,2,128]{3,1,2,0:T(8,128)(2,1)} %bitcast.225, bf16[128,2,6,64]{3,2,1,0:T(8,128)(2,1)S(1)} %copy.96, bf16[128,2,6,64]{3,2,1,0:T(8,128)(2,1)S(1)} %copy.95, pred[128,128]{1,0:T(8,128)(4,1)S(1)} %iota_compare_fusion.3), kind=kOutput, calls=%fused_computation.260 | convolution fusion | flops 51706368 | bytes 9590784 | tf_op jit(solution)/shard_map/cond/branch_1_fun/nkgd,nskd->nkgs/dot_general | solution.py:38
  459.1 1.8 copy.110
  465.1 5.7 fusion.117
  471.2 3.9 fusion.120
  475.1 1.9 fusion.121
  478.4 1.4 gather_fusion.8
  482.4 1.4 scatter_custom_fusion.2
  483.8 4.7 gather_fusion.9
  489.7 1.4 scatter_custom_fusion.3
  491.4 21.0 %all_to_all.72 = bf16[8,48,1536]{2,1,0:T(8,128)(2,1)S(1)} all-to-all(bf16[8,48,1536]{2,1,0:T(8,128)(2,1)} %bitcast.69), channel_id=1, replica_groups=mesh['dp'=1,'pool'=4,'ep'=8] {'ep'}, dimensions={0} | all-to-all | bytes 2359296 | tf_op jit(solution)/shard_map/all_to_all | solution.py:151
  512.4 1.4 collective-permute-start.5
  513.8 7.9 %all_to_all.73 = s32[8,48,1]{1,2,0:T(1,128)S(1)} all-to-all(s32[8,48,1]{1,2,0:T(1,128)S(1)} %bitcast.243), channel_id=1, replica_groups=mesh['dp'=1,'pool'=4,'ep'=8] {'ep'}, dimensions={0} | all-to-all | bytes 3072 | tf_op jit(solution)/shard_map/all_to_all | solution.py:152
  523.7 14.7 %collective-permute-done.4 = s32[384]{0:T(512)S(1)} collective-permute-done((s32[384]{0:T(512)S(1)}, s32[384]{0:T(512)S(1)}, u32[]{:S(2)}, u32[]{:S(2)}) %collective-permute-start.4) | collective-permute-done | bytes 1568 | tf_op jit(solution)/shard_map/ppermute | solution.py:152
  539.8 119.2 %collective-permute-done.6 = bf16[384,1536]{1,0:T(8,128)(2,1)} collective-permute-done((bf16[384,1536]{1,0:T(8,128)(2,1)S(1)}, bf16[384,1536]{1,0:T(8,128)(2,1)}, u32[]{:S(2)}, u32[]{:S(2)}) %collective-permute-start.6) | collective-permute-done | bytes 1179680 | tf_op jit(solution)/shard_map/ppermute | solution.py:154
  659.1 6.1 all-to-all-start.5
  665.2 16.3 %all-to-all-done.5 = bf16[8,48,1536]{2,1,0:T(8,128)(2,1)S(1)} async-done(((bf16[8,48,1536]{2,1,0:T(8,128)(2,1)}), bf16[8,48,1536]{2,1,0:T(8,128)(2,1)S(1)}, u32[]{:S(2)}, u32[]{:S(2)}) %all-to-all-start.5) | async-done | bytes 1179680 | tf_op jit(solution)/shard_map/all_to_all | solution.py:154
  681.4 21.7 %conditional.11 = (bf16[128,1536]{1,0:T(8,128)(2,1)S(1)}) conditional(s32[]{:T(128)} %convert_element_type.170, () %tuple.49, (bf16[128,1536]{1,0:T(8,128)(2,1)}, f32[128,2]{1,0:T(8,128)}, bf16[8,48,1536]{2,1,0:T(8,128)(2,1)S(1)}, s32[256]{0:T(256)S(1)}, bf16[2,1536,4096]{2,1,0:T(8,128)(2,1)}, /*index=5*/bf16[128,1536]{1,0:T(8,128)(2,1)}, ...), branch_computations={%region_39.44_spmd, %region_40.46_spmd} | conditional | flops 4837542912 | bytes 53750280 | solution.py:155
  683.8 3.1 multiply_reduce_fusion.1
  686.9 5.7 fusion.38
  692.7 10.5 %fusion.58 = bf16[128,1536]{1,0:T(8,128)(2,1)S(1)} fusion(bf16[2,4096,1536]{2,1,0:T(8,128)(2,1)} %get-tuple-element.176, f32[128,1536]{1,0:T(8,128)S(1)} %multiply_reduce_fusion.1, bf16[128,1536]{1,0:T(8,128)(2,1)} %get-tuple-element.169, bf16[128,1536]{1,0:T(8,128)(2,1)} %get-tuple-element.173, bf16[2,1536,4096]{2,1,0:T(8,128)(2,1)} %get-tuple-element.175, ...), kind=kOutput, calls=%fused_computation.81 | convolution fusion | flops 3225550848 | bytes 29229056 | tf_op jit(solution)/shard_map/cond/branch_1_fun/dot_general | solution.py:62
  704.5 3.3 collective-permute-done.7
  (170 shorter events, 43.7 us)
Async XLA Ops:
  0.0 10.3 %collective-permute-start = (bf16[64,1536]{1,0:T(8,128)(2,1)}, bf16[64,1536]{1,0:T(8,128)(2,1)S(1)}, u32[]{:S(2)}, u32[]{:S(2)}) collective-permute-start(bf16[64,1536]{1,0:T(8,128)(2,1)} %param.36), channel_id=1, source_target_pairs={{16,0},{24,8},{17,1},{25,9},{18,2},{26,10},{19,3},{27,11},{20,4},{... | collective-permute-start | bytes 589832 | tf_op jit(solution)/shard_map/ppermute | solution.py:147
  25.4 16.5 %copy-start = (bf16[1,256,128,2,128]{4,3,2,1,0:T(2,128)(2,1)S(1)}, bf16[1,256,128,2,128]{4,3,2,1,0:T(2,128)(2,1)}, u32[]{:S(2)}) copy-start(bf16[1,256,128,2,128]{4,3,2,1,0:T(2,128)(2,1)} %slice.95) | copy-start | bytes 50331652 | tf_op jit(solution)/shard_map/cond
  89.6 2.3 slice-start
  94.8 9.1 %copy-start.10 = (bf16[2,1536,256]{2,1,0:T(8,128)(2,1)S(1)}, bf16[2,1536,256]{2,1,0:T(8,128)(2,1)}, u32[]{:S(2)}) copy-start(bf16[2,1536,256]{2,1,0:T(8,128)(2,1)} %get-tuple-element.131) | copy-start | bytes 4718596 | tf_op jit(solution)/shard_map/cond
  94.8 11.1 %copy-start.3 = (bf16[2,1536,256]{2,1,0:T(8,128)(2,1)S(1)}, bf16[2,1536,256]{2,1,0:T(8,128)(2,1)}, u32[]{:S(2)}) copy-start(bf16[2,1536,256]{2,1,0:T(8,128)(2,1)} %get-tuple-element.327) | copy-start | bytes 4718596 | tf_op jit(solution)/shard_map/cond
  108.0 3.0 copy-start.4
  117.9 6.2 copy-start.6
  160.6 26.1 %collective-permute-start.2 = (bf16[384,1536]{1,0:T(8,128)(2,1)S(1)}, bf16[384,1536]{1,0:T(8,128)(2,1)S(1)}, u32[]{:S(2)}, u32[]{:S(2)}) collective-permute-start(bf16[384,1536]{1,0:T(8,128)(2,1)S(1)} %bitcast.235), channel_id=1, source_target_pairs={{0,16},{8,24},{1,17},{9,25},{2,18},{10,26},{3,19},{11,27},{4,20},{... | collective-permute-start | bytes 3538952 | tf_op jit(solution)/shard_map/ppermute | solution.py:151
  170.7 16.0 %collective-permute-start.1 = (s32[384]{0:T(512)S(1)}, s32[384]{0:T(512)S(1)}, u32[]{:S(2)}, u32[]{:S(2)}) collective-permute-start(s32[384]{0:T(512)S(1)} %all_to_all.50), channel_id=1, source_target_pairs={{0,16},{8,24},{1,17},{9,25},{2,18},{10,26},{3,19},{11,27},{4,20},{... | collective-permute-start | bytes 4616 | tf_op jit(solution)/shard_map/ppermute | solution.py:152
  186.8 123.9 %collective-permute-start.3 = (bf16[384,1536]{1,0:T(8,128)(2,1)S(1)}, bf16[384,1536]{1,0:T(8,128)(2,1)}, u32[]{:S(2)}, u32[]{:S(2)}) collective-permute-start(bf16[384,1536]{1,0:T(8,128)(2,1)S(1)} %get-tuple-element.411), channel_id=1, source_target_pairs={{16,0},{24,8},{17,1},{25,9},{18,2},{26,10},{19,3},{27,11},{20,4},{... | collective-permute-start | bytes 3538952 | tf_op jit(solution)/shard_map/ppermute | solution.py:154
  310.7 23.1 %all-to-all-start.2 = ((bf16[8,48,1536]{2,1,0:T(8,128)(2,1)}), bf16[8,48,1536]{2,1,0:T(8,128)(2,1)S(1)}, u32[]{:S(2)}, u32[]{:S(2)}) async-start(bf16[8,48,1536]{2,1,0:T(8,128)(2,1)} %bitcast.67), calls=%async_computation.2 | async-start | bytes 2359296 | tf_op jit(solution)/shard_map/all_to_all | solution.py:154
  333.8 30.3 %copy-start.2 = (bf16[2,1536,256]{2,1,0:T(8,128)(2,1)S(1)}, bf16[2,1536,256]{2,1,0:T(8,128)(2,1)}, u32[]{:S(2)}) copy-start(bf16[2,1536,256]{2,1,0:T(8,128)(2,1)} %param.41) | copy-start | bytes 4718596
  364.5 14.2 %copy-start.8 = (s32[2,64]{1,0:T(2,128)}, s32[2,64]{1,0:T(2,128)S(1)}, u32[]{:S(2)}) copy-start(s32[2,64]{1,0:T(2,128)S(1)} %get-tuple-element.151) | copy-start | bytes 1540 | tf_op jit(solution)/shard_map/cond
  378.7 16.5 %copy-start.1 = (bf16[1,256,128,2,128]{4,3,2,1,0:T(2,128)(2,1)S(1)}, bf16[1,256,128,2,128]{4,3,2,1,0:T(2,128)(2,1)}, u32[]{:S(2)}) copy-start(bf16[1,256,128,2,128]{4,3,2,1,0:T(2,128)(2,1)} %slice.116) | copy-start | bytes 50331652 | tf_op jit(solution)/shard_map/cond
  442.9 2.3 slice-start.1
  442.9 5.0 copy-start.9
  448.1 9.0 %copy-start.11 = (bf16[2,1536,256]{2,1,0:T(8,128)(2,1)S(1)}, bf16[2,1536,256]{2,1,0:T(8,128)(2,1)}, u32[]{:S(2)}) copy-start(bf16[2,1536,256]{2,1,0:T(8,128)(2,1)} %get-tuple-element.158) | copy-start | bytes 4718596 | tf_op jit(solution)/shard_map/cond
  460.9 3.0 copy-start.5
  470.8 6.2 copy-start.7
  512.4 26.1 %collective-permute-start.5 = (bf16[384,1536]{1,0:T(8,128)(2,1)S(1)}, bf16[384,1536]{1,0:T(8,128)(2,1)S(1)}, u32[]{:S(2)}, u32[]{:S(2)}) collective-permute-start(bf16[384,1536]{1,0:T(8,128)(2,1)S(1)} %bitcast.234), channel_id=1, source_target_pairs={{0,16},{8,24},{1,17},{9,25},{2,18},{10,26},{3,19},{11,27},{4,20},{... | collective-permute-start | bytes 3538952 | tf_op jit(solution)/shard_map/ppermute | solution.py:151
  522.4 16.0 %collective-permute-start.4 = (s32[384]{0:T(512)S(1)}, s32[384]{0:T(512)S(1)}, u32[]{:S(2)}, u32[]{:S(2)}) collective-permute-start(s32[384]{0:T(512)S(1)} %all_to_all.58), channel_id=1, source_target_pairs={{0,16},{8,24},{1,17},{9,25},{2,18},{10,26},{3,19},{11,27},{4,20},{... | collective-permute-start | bytes 4616 | tf_op jit(solution)/shard_map/ppermute | solution.py:152
  538.5 120.5 %collective-permute-start.6 = (bf16[384,1536]{1,0:T(8,128)(2,1)S(1)}, bf16[384,1536]{1,0:T(8,128)(2,1)}, u32[]{:S(2)}, u32[]{:S(2)}) collective-permute-start(bf16[384,1536]{1,0:T(8,128)(2,1)S(1)} %get-tuple-element.413), channel_id=1, source_target_pairs={{16,0},{24,8},{17,1},{25,9},{18,2},{26,10},{19,3},{27,11},{20,4},{... | collective-permute-start | bytes 3538952 | tf_op jit(solution)/shard_map/ppermute | solution.py:154
  659.1 22.4 %all-to-all-start.5 = ((bf16[8,48,1536]{2,1,0:T(8,128)(2,1)}), bf16[8,48,1536]{2,1,0:T(8,128)(2,1)S(1)}, u32[]{:S(2)}, u32[]{:S(2)}) async-start(bf16[8,48,1536]{2,1,0:T(8,128)(2,1)} %bitcast.71), calls=%async_computation.5 | async-start | bytes 2359296 | tf_op jit(solution)/shard_map/all_to_all | solution.py:154
  703.2 4.6 collective-permute-start.7
where the time goes:
time: 720 us; the launch traced here: 709 us
  waiting for transfers between devices  313 us (43%)
  local copies, waits for them, and re-layouts  204 us (28%)
  matrix products  80.7 us (11%)
  blocking collectives  59.6 us (8%)
  other arithmetic  25.9 us (4%)
  starting transfers between devices  23.6 us (3%)
    ppermute x2, waiting for transfers between devices, body(): lax.ppermute(expert_out, 'pool', to_att)  242 us
    all_to_all x2, blocking collectives, body(): lax.all_to_all(send_rows, 'ep', 0, 0, tiled=True)  43.8 us
    cond x28, local copies, waits for them, and re-layouts  41.6 us
    dynamic_slice x5, local copies, waits for them, and re-layouts, my_rows(): lax.dynamic_index_in_dim(split, sub_idx, axis=axis + 1, keepdims=False)  34.1 us
    all_to_all x2, waiting for transfers between devices, body(): lax.all_to_all(lax.ppermute(expert_out, 'pool', to_att), 'ep', 0, 0, tile...  32.4 us
    another operation x9, local copies, waits for them, and re-layouts  29.6 us
    ppermute x2, waiting for transfers between devices, body(): lax.ppermute(lax.all_to_all(send_loc, 'ep', 0, 0, tiled=True), 'pool', to...  29.4 us
    slice x2, local copies, waits for them, and re-layouts, attention_stage(): k_cache[layer]  28.6 us
  transfers between devices with their start and end apart: 10, of which 8 were waited for; matrix products, arithmetic and copies ran while one was open for 1% of the time, Pallas kernels for 0%

commit v1 on v0

v1 whole, which is shorter than its diff:
```python
import functools
import math
import jax
import jax.numpy as jnp
from jax import lax
from jax.experimental import pallas as pl
from jax.experimental.pallas import tpu as pltpu
from jax.sharding import PartitionSpec as P

RMS_EPS = 1e-6
ROPE_BASE = 10000.0
MESH = pl.DeviceIdType.MESH
BF16 = jnp.bfloat16
F32 = jnp.float32
ANY = pl.BlockSpec(memory_space=pl.ANY)
VMEM = pl.BlockSpec(memory_space=pltpu.VMEM)
SMEM = pl.BlockSpec(memory_space=pltpu.SMEM)
VMEM_BYTES = 66_000_000
META = 128
TOK_STEP = 8
FF_CHUNK = 512
RING = 8


def rms(vals):
    return vals * lax.rsqrt(jnp.mean(vals * vals, axis=-1, keepdims=True) + RMS_EPS)


def mm(lhs, rhs):
    return jnp.dot(lhs, rhs, preferred_element_type=F32)


def silu(vals):
    return vals * (1.0 / (1.0 + jnp.exp(-vals)))


def attention_kernel(layer, capacity, q_heads, kv_heads, lens, x_ref, cos_ref, sin_ref, ids_ref, wr_ref, wq, wk, wv, wo, kc, vc,
                     a_ref, u_ref, meta_ref, wq_b, wk_b, wv_b, wo_b, k_b, v_b, q3, kn3, vn3, o3, attn, w_sem, k_sem, v_sem):
    n_tok, d_model = x_ref.shape
    rows = kc.shape[2]
    head_dim = kc.shape[3]
    group = q_heads // kv_heads
    steps = n_tok // TOK_STEP
    first = lax.axis_index("pool") * n_tok
    scale = head_dim ** -0.5
    weights = [(wq, wq_b), (wk, wk_b), (wv, wv_b), (wo, wo_b)]
    w_copies = [pltpu.make_async_copy(src.at[layer], dst, w_sem.at[i]) for i, (src, dst) in enumerate(weights)]

    def cache_copies(step):
        here = pl.ds(step * TOK_STEP, TOK_STEP)
        there = pl.ds(first + step * TOK_STEP, TOK_STEP)
        return (pltpu.make_async_copy(kc.at[layer, there], k_b.at[here], k_sem.at[step]),
                pltpu.make_async_copy(vc.at[layer, there], v_b.at[here], v_sem.at[step]))

    for copy in w_copies[:3]:
        copy.start()
    for step in range(steps):
        for copy in cache_copies(step):
            copy.start()
    w_copies[3].start()

    q3[...] = jnp.zeros_like(q3)
    kn3[...] = jnp.zeros_like(kn3)
    vn3[...] = jnp.zeros_like(vn3)
    x_f = x_ref[...].astype(F32)
    hidden = rms(x_f).astype(BF16)
    cosine = cos_ref[...]
    sine = sin_ref[...]

    def rotated(vals):
        return (vals * cosine + pltpu.roll(vals, head_dim // 2, 1) * sine).astype(BF16).astype(F32)

    w_copies[0].wait()
    query = mm(hidden, wq_b[...])
    for head in range(q_heads):
        q3[:, head, :] = rotated(query[:, head * head_dim:(head + 1) * head_dim])
    w_copies[1].wait()
    key = mm(hidden, wk_b[...])
    w_copies[2].wait()
    val = mm(hidden, wv_b[...]).astype(BF16).astype(F32)
    for kv in range(kv_heads):
        cols = slice(kv * head_dim, (kv + 1) * head_dim)
        key_rot = rotated(key[:, cols])
        for head in range(kv * group, (kv + 1) * group):
            kn3[:, head, :] = key_rot
            vn3[:, head, :] = val[:, cols]

    pad = q3.shape[1]
    lane = lax.broadcasted_iota(jnp.int32, (pad, rows), 1)
    head_kv = lax.broadcasted_iota(jnp.int32, (pad, rows), 0) // group
    right_kv = lane % kv_heads == head_kv
    position = lane // kv_heads

    def step_body(step, carry):
        for copy in cache_copies(step):
            copy.wait()
        base = step * TOK_STEP
        q_f = q3[pl.ds(base, TOK_STEP)]
        scores = lax.dot_general(q_f.astype(BF16), k_b[pl.ds(base, TOK_STEP)], (((2,), (2,)), ((0,), (0,))), preferred_element_type=F32)
        s_new = jnp.sum(q_f * kn3[pl.ds(base, TOK_STEP)], axis=-1, keepdims=True) * scale
        probs = []
        p_news = []
        for i in range(TOK_STEP):
            valid = right_kv & (position < lens[base + i])
            s_i = jnp.where(valid, scores[i] * scale, -jnp.inf)
            peak = jnp.maximum(jnp.max(s_i, axis=-1, keepdims=True), s_new[i])
            e_i = jnp.exp(s_i - peak)
            e_new = jnp.exp(s_new[i] - peak)
            total = jnp.sum(e_i, axis=-1, keepdims=True) + e_new
            probs.append((e_i / total).astype(BF16))
            p_news.append((e_new / total).astype(BF16).astype(F32))
        for i in range(TOK_STEP):
            mixed = mm(probs[i], v_b[base + i])
            o3[base + i] = mixed + p_news[i] * vn3[base + i]
        return carry

    lax.fori_loop(0, steps, step_body, 0)
    for head in range(q_heads):
        attn[:, head * head_dim:(head + 1) * head_dim] = o3[:, head, :].astype(BF16)
    w_copies[3].wait()
    resid = (x_f + mm(attn[...], wo_b[...])).astype(BF16)
    a_ref[...] = resid
    normed = rms(resid.astype(F32)).astype(BF16)
    u_ref[:, :d_model] = normed

    logits = lax.dot_general(normed.astype(F32), wr_ref[...], (((1,), (1,)), ((), ())), precision=lax.Precision.HIGHEST, preferred_element_type=F32)
    experts = logits.shape[1]
    lane_e = lax.broadcasted_iota(jnp.int32, (n_tok, META), 1)
    id0 = ids_ref[:, 0:1]
    id1 = ids_ref[:, 1:2]
    pick0 = lane_e == id0
    pick1 = lane_e == id1
    l0 = jnp.sum(jnp.where(pick0[:, :experts], logits, 0.0), axis=-1, keepdims=True)
    l1 = jnp.sum(jnp.where(pick1[:, :experts], logits, 0.0), axis=-1, keepdims=True)
    peak = jnp.maximum(l0, l1)
    e0 = jnp.exp(l0 - peak)
    e1 = jnp.exp(l1 - peak)
    member = jnp.where(pick0 | pick1, 1.0, 0.0)
    earlier = jnp.where(lax.broadcasted_iota(jnp.int32, (n_tok, n_tok), 1) < lax.broadcasted_iota(jnp.int32, (n_tok, n_tok), 0), 1.0, 0.0)
    rank = mm(earlier.astype(BF16), member.astype(BF16))
    u_ref[:, d_model:] = jnp.where(member > 0.0, rank, -1.0).astype(BF16)
    slot0 = id0.astype(F32) * capacity + jnp.sum(jnp.where(pick0, rank, 0.0), axis=-1, keepdims=True)
    slot1 = id1.astype(F32) * capacity + jnp.sum(jnp.where(pick1, rank, 0.0), axis=-1, keepdims=True)
    total = e0 + e1
    meta_ref[...] = jnp.where(lane_e == 0, slot0, jnp.where(lane_e == 1, slot1, jnp.where(lane_e == 2, e0 / total, e1 / total)))


def moe_kernel(layer, capacity, ep_size, u_ref, a_ref, meta_ref, sg, su, sd, wg, wu, wd, out_ref,
               gath, back, picked, sent, acc_e, acc_s, g_b, u_b, d_b, w_sem, ag_send, ag_recv, ret_send, ret_recv):
    n_tok = a_ref.shape[0]
    d_model = a_ref.shape[1]
    half = n_tok // 2
    n_chunks = sg.shape[2] // FF_CHUNK
    me = lax.axis_index("ep")
    partner = me + 1 - 2 * lax.rem(me, 2)
    right = lax.rem(me + 2, ep_size)
    left = lax.rem(me + ep_size - 2, ep_size)
    far = lax.rem(me + ep_size // 2, ep_size)

    def weight_copies(chunk, slot, shared):
        cols = pl.ds(chunk * FF_CHUNK, FF_CHUNK)
        if shared:
            srcs = (sg.at[layer, :, cols], su.at[layer, :, cols], sd.at[layer, cols])
        else:
            srcs = (wg.at[layer, 0, :, cols], wu.at[layer, 0, :, cols], wd.at[layer, 0, cols])
        dsts = (g_b.at[slot], u_b.at[slot], d_b.at[slot])
        return [pltpu.make_async_copy(src, dst, w_sem.at[slot, i]) for i, (src, dst) in enumerate(zip(srcs, dsts))]

    for chunk in range(RING):
        for copy in weight_copies(chunk, chunk, True):
            copy.start()

    barrier = pltpu.get_barrier_semaphore()
    for other in range(1, ep_size):
        pl.semaphore_signal(barrier, inc=1, device_id={"ep": lax.rem(me + other, ep_size)}, device_id_type=MESH)
    gath[me] = u_ref[...]
    pl.semaphore_wait(barrier, ep_size - 1)

    def piece(src, part):
        return gath.at[src, pl.ds(part * half, half)]

    def gather_copy(src, part, where, target, from_input=False):
        ref = u_ref.at[pl.ds(part * half, half)] if from_input else piece(src, part)
        return pltpu.make_async_remote_copy(src_ref=ref, dst_ref=piece(src, part), send_sem=ag_send.at[where], recv_sem=ag_recv.at[src, part],
                                            device_id={"ep": target}, device_id_type=MESH)

    def arrived(src, part):
        pltpu.make_async_remote_copy(src_ref=piece(src, part), dst_ref=piece(src, part), send_sem=ag_send.at[0], recv_sem=ag_recv.at[src, part],
                                     device_id={"ep": partner}, device_id_type=MESH).wait_recv()

    sends = []

    def send(src, part, target, from_input=False):
        copy = gather_copy(src, part, len(sends), target, from_input)
        copy.start()
        sends.append(copy)

    send(me, 0, right, True)
    send(me, 1, left, True)
    send(me, 1, right, True)
    send(me, 0, left, True)
    send(me, 0, partner, True)
    send(me, 1, partner, True)

    acc_s[...] = jnp.zeros_like(acc_s)
    acc_e[...] = jnp.zeros_like(acc_e)

    def chunk_mlp(rows, slot):
        mid = (silu(mm(rows, g_b[slot])) * mm(rows, u_b[slot])).astype(BF16)
        return mm(mid, d_b[slot])

    def shared_step(chunk, carry):
        slot = lax.rem(chunk, RING)
        for copy in weight_copies(chunk, slot, True):
            copy.wait()
        acc_s[...] += chunk_mlp(u_ref[:, :d_model], slot)
        for copy in weight_copies(chunk, slot, False):
            copy.start()
        return carry

    lax.fori_loop(0, 3, shared_step, 0)
    arrived(left, 0)
    send(left, 0, right)
    arrived(right, 1)
    send(right, 1, left)
    send(left, 0, partner)
    send(right, 1, partner)
    lax.fori_loop(3, 5, shared_step, 0)
    for src, part in ((left, 1), (right, 0)):
        arrived(src, part)
        send(src, part, partner)
    lax.fori_loop(5, 7, shared_step, 0)
    for src, part in ((far, 0), (far, 1)):
        arrived(src, part)
        send(src, part, partner)
    lax.fori_loop(7, n_chunks, shared_step, 0)
    for hop in (0, 2, ep_size - 2, ep_size // 2):
        for part in (0, 1):
            arrived(lax.rem(partner + hop, ep_size), part)

    lane = lax.broadcasted_iota(jnp.int32, (n_tok, META), 1)

    def pick_step(src, carry):
        codes = gath[src, :, d_model:].astype(F32)
        rank = jnp.sum(jnp.where(lane == me, codes, 0.0), axis=-1, keepdims=True)
        choose = jnp.where(lane.astype(F32) == rank, 1.0, 0.0).astype(BF16)
        rows = lax.dot_general(choose, gath[src, :, :d_model], (((0,), (0,)), ((), ())), preferred_element_type=F32)
        picked[pl.ds(src * capacity, capacity)] = rows[:capacity].astype(BF16)
        return carry

    lax.fori_loop(0, ep_size, pick_step, 0)

    def expert_step(chunk, carry):
        slot = lax.rem(chunk, RING)
        for copy in weight_copies(chunk, slot, False):
            copy.wait()
        acc_e[...] += chunk_mlp(picked[...], slot)
        return carry

    lax.fori_loop(0, n_chunks, expert_step, 0)
    for src in range(ep_size):
        sent[src] = acc_e[pl.ds(src * capacity, capacity)].astype(BF16)

    def return_copy(hop):
        target = lax.rem(me + hop, ep_size)
        return pltpu.make_async_remote_copy(src_ref=sent.at[target], dst_ref=back.at[me], send_sem=ret_send.at[hop], recv_sem=ret_recv.at[me],
                                            device_id={"ep": target}, device_id_type=MESH)

    order = [ep_size // 2, ep_size // 2 + 1, 2, 3, ep_size - 2, ep_size - 1, 1]
    for hop in order:
        return_copy(hop).start()
    back[me] = sent[me]
    for copy in sends:
        copy.wait_send()
    for hop in order:
        return_copy(hop).wait_send()
        src = lax.rem(me + hop, ep_size)
        pltpu.make_async_remote_copy(src_ref=back.at[src], dst_ref=back.at[src], send_sem=ret_send.at[hop], recv_sem=ret_recv.at[src],
                                     device_id={"ep": src}, device_id_type=MESH).wait_recv()

    slot_lane = lax.broadcasted_iota(jnp.int32, (n_tok, ep_size * capacity), 1).astype(F32)
    table = back[...].reshape(ep_size * capacity, d_model)
    y0 = mm(jnp.where(slot_lane == meta_ref[:, 0:1], 1.0, 0.0).astype(BF16), table)
    y1 = mm(jnp.where(slot_lane == meta_ref[:, 1:2], 1.0, 0.0).astype(BF16), table)
    routed = meta_ref[:, 2:3] * y0 + meta_ref[:, 3:4] * y1
    out_ref[...] = (a_ref[...].astype(F32) + routed + acc_s[...].astype(BF16).astype(F32)).astype(BF16)


def solution(mesh):
    ep_size = mesh.shape["ep"]
    row_spec = P(("dp", "ep", "pool"), None)
    cache_spec = P(None, ("dp", "ep"), None, None, None)
    expert_spec = P(None, "ep", None, None)
    in_specs = (row_spec, cache_spec, cache_spec, P(("dp", "ep")), P(), P(), P(), P(), P(), P(None, ("dp", "ep"), None), expert_spec, expert_spec, expert_spec, P(), P(), P())

    def body(x_loc, k_cache, v_cache, cache_len, w_query, w_key, w_value, w_out, w_router, expert_ids, w_gate, w_up, w_down, shared_gate, shared_up, shared_down):
        n_tok, d_model = x_loc.shape
        n_layers, all_tok, ctx, kv_heads, head_dim = k_cache.shape
        q_heads = w_query.shape[2] // head_dim
        top_k = expert_ids.shape[2]
        capacity = 3 * n_tok * top_k // ep_size
        rows = ctx * kv_heads
        pad_heads = -(-q_heads // 8) * 8
        first = lax.axis_index("pool") * n_tok
        lens = lax.dynamic_slice_in_dim(cache_len, first, n_tok, 0)
        ids = lax.dynamic_slice_in_dim(expert_ids, first, n_tok, 1)
        half = head_dim // 2
        inv_freq = jnp.exp(jnp.arange(half, dtype=F32) * (-math.log(ROPE_BASE) / half))
        angle = lens.astype(F32)[:, None] * inv_freq
        cosine = jnp.cos(angle)
        sine = jnp.sin(angle)
        cos2 = jnp.concatenate([cosine, cosine], axis=1)
        sin2 = jnp.concatenate([-sine, sine], axis=1)
        router_t = jnp.swapaxes(w_router, 1, 2)
        k_rows = k_cache.reshape(n_layers, all_tok, rows, head_dim)
        v_rows = v_cache.reshape(n_layers, all_tok, rows, head_dim)
        ext = d_model + META
        x_cur = x_loc
        for layer in range(n_layers):
            resid, u_ext, meta = pl.pallas_call(
                functools.partial(attention_kernel, layer, capacity, q_heads, kv_heads),
                name=f"attention_{layer}",
                out_shape=(jax.ShapeDtypeStruct((n_tok, d_model), BF16), jax.ShapeDtypeStruct((n_tok, ext), BF16), jax.ShapeDtypeStruct((n_tok, META), F32)),
                in_specs=[SMEM] + [VMEM] * 5 + [ANY] * 6,
                out_specs=(VMEM, VMEM, VMEM),
                scratch_shapes=[
                    pltpu.VMEM(w_query.shape[1:], BF16), pltpu.VMEM(w_key.shape[1:], BF16), pltpu.VMEM(w_value.shape[1:], BF16), pltpu.VMEM(w_out.shape[1:], BF16),
                    pltpu.VMEM((n_tok, rows, head_dim), BF16), pltpu.VMEM((n_tok, rows, head_dim), BF16),
                    pltpu.VMEM((n_tok, pad_heads, head_dim), F32), pltpu.VMEM((n_tok, pad_heads, head_dim), F32),
                    pltpu.VMEM((n_tok, pad_heads, head_dim), F32), pltpu.VMEM((n_tok, pad_heads, head_dim), F32),
                    pltpu.VMEM((n_tok, q_heads * head_dim), BF16),
                    pltpu.SemaphoreType.DMA((4,)), pltpu.SemaphoreType.DMA((n_tok // TOK_STEP,)), pltpu.SemaphoreType.DMA((n_tok // TOK_STEP,)),
                ],
                compiler_params=pltpu.CompilerParams(vmem_limit_bytes=VMEM_BYTES),
            )(lens, x_cur, cos2, sin2, ids[layer], router_t[layer], w_query, w_key, w_value, w_out, k_rows, v_rows)
            d_ff = shared_gate.shape[2]
            x_cur = pl.pallas_call(
                functools.partial(moe_kernel, layer, capacity, ep_size),
                name=f"moe_{layer}",
                out_shape=jax.ShapeDtypeStruct((n_tok, d_model), BF16),
                in_specs=[VMEM] * 3 + [ANY] * 6,
                out_specs=VMEM,
                scratch_shapes=[
                    pltpu.VMEM((ep_size, n_tok, ext), BF16), pltpu.VMEM((ep_size, capacity, d_model), BF16),
                    pltpu.VMEM((ep_size * capacity, d_model), BF16), pltpu.VMEM((ep_size, capacity, d_model), BF16),
                    pltpu.VMEM((ep_size * capacity, d_model), F32), pltpu.VMEM((n_tok, d_model), F32),
                    pltpu.VMEM((RING, d_model, FF_CHUNK), BF16), pltpu.VMEM((RING, d_model, FF_CHUNK), BF16), pltpu.VMEM((RING, FF_CHUNK, d_model), BF16),
                    pltpu.SemaphoreType.DMA((RING, 3)), pltpu.SemaphoreType.DMA((14,)), pltpu.SemaphoreType.DMA((ep_size, 2)),
                    pltpu.SemaphoreType.DMA((ep_size,)), pltpu.SemaphoreType.DMA((ep_size,)),
                ],
                compiler_params=pltpu.CompilerParams(vmem_limit_bytes=VMEM_BYTES, collective_id=layer, has_side_effects=True),
            )(u_ext, resid, meta, shared_gate, shared_up, shared_down, w_gate, w_up, w_down)
        return x_cur

    return jax.shard_map(body, mesh=mesh, in_specs=in_specs, out_specs=row_spec, check_vma=False)
```

time: 720 us -> 140 us (0.19); the launches traced: 709 us -> 139 us
  waiting for transfers between devices: 313 us -> 0 us
  local copies, waits for them, and re-layouts: 204 us -> 5.27 us
  Pallas kernels: 0 us -> 132 us
  matrix products: 80.7 us -> 0 us
  blocking collectives: 59.6 us -> 0 us
  other arithmetic: 25.9 us -> 2.2 us
  starting transfers between devices: 23.6 us -> 0 us
    ppermute x8 -> x0, waiting for transfers between devices: 281 us -> none  [the longest x2 242 us: body(): lax.ppermute(expert_out, 'pool', to_att)]
    pallas_call x0 -> x4, Pallas kernels: none -> 132 us  [the longest x2 103 us: body(): pl.pallas_call(functools.partial(moe_kernel, layer, capacity, ep_size), n...]
    dot_general x18 -> x0, matrix products: 80.7 us -> none  [the longest x2 21.6 us: gated_mlp(): jnp.dot(mid, w_down, preferred_element_type=jnp.float32)]
    slice x12 -> x0, local copies, waits for them, and re-layouts: 64 us -> none  [the longest x2 28.6 us: attention_stage(): k_cache[layer]]
    all_to_all x4 -> x0, blocking collectives: 59.6 us -> none  [the longest x2 43.8 us: body(): lax.all_to_all(send_rows, 'ep', 0, 0, tiled=True)]
    cond x28 -> x0, local copies, waits for them, and re-layouts: 41.6 us -> none
    dynamic_slice x5 -> x0, local copies, waits for them, and re-layouts: 34.1 us -> none  [my_rows(): lax.dynamic_index_in_dim(split, sub_idx, axis=axis + 1, keepdims=False)]
    all_to_all x2 -> x0, waiting for transfers between devices: 32.4 us -> none  [body(): lax.all_to_all(lax.ppermute(expert_out, 'pool', to_att), 'ep', 0, 0, tile...]
  transfers between devices with their start and end apart: 10 -> 0, of which waited for: 8 -> 0; matrix products, arithmetic and copies ran while one was open for 1% -> 0% of each run, Pallas kernels for 0% -> 0%
where the time goes in v1:
time: 140 us; the launch traced here: 139 us
  Pallas kernels  132 us (94%)
  local copies, waits for them, and re-layouts  5.27 us (4%)
  other arithmetic  2.2 us (2%)
    pallas_call x2, Pallas kernels, body(): pl.pallas_call(functools.partial(moe_kernel, layer, capacity, ep_size), n...  103 us
    pallas_call x2, Pallas kernels, body(): pl.pallas_call(functools.partial(attention_kernel, layer, capacity, q_hea...  28.7 us

profile of v1, /device:TPU:97, one launch (start us, length us, event | category | flops | bytes accessed | tf_op | source)
XLA Modules:
  0.0 139.3 jit_solution(7615598714593796516)
XLA Ops:
  0.0 1.3 fusion.1
  1.3 0.8 dynamic-slice_bitcast_fusion
  2.1 0.7 copy.18.ids_ref
  2.8 0.7 copy.17.ids_ref
  3.5 0.2 fusion
  3.7 0.7 pad_maximum_fusion
  4.4 1.5 %slice_bitcast_fusion = (f32[8,1536]{1,0:T(8,128)}, f32[8,1536]{1,0:T(8,128)}) fusion(f32[2,8,1536]{2,1,0:T(8,128)} %bitcast.15), kind=kLoop, calls=%fused_computation | loop fusion | bytes 196608 | tf_op jit(solution)/shard_map/squeeze | solution.py:335
  5.9 14.3 %attention_0.1 = (bf16[64,1536]{1,0:T(8,128)(2,1)}, bf16[64,1664]{1,0:T(8,128)(2,1)}, f32[64,128]{1,0:T(8,128)}) custom-call(s32[64]{0:T(128)} %get-tuple-element.18.lens, bf16[64,1536]{1,0:T(8,128)(2,1)} %x_ref.1, f32[64,128]{1,0:T(8,128)} %get-tuple-element.26.cos_ref, f32[64,128]{1,0:T(8,128)} %get-tuple-element.27.sin_ref, s32[64,2]{1,0:T(8,128)} %copy.17.ids_ref, ...), custom_call_target="tpu_custom_call" | custom-call | tf_op jit(solution)/shard_map/attention_0/pallas_call | solution.py:320
  20.2 53.0 %moe_0.1.x_ref = bf16[64,1536]{1,0:T(8,128)(2,1)} custom-call(bf16[64,1664]{1,0:T(8,128)(2,1)} %get-tuple-element.11.u_ref, bf16[64,1536]{1,0:T(8,128)(2,1)} %get-tuple-element.12.a_ref, f32[64,128]{1,0:T(8,128)} %get-tuple-element.13.meta_ref, bf16[2,1536,4096]{2,1,0:T(8,128)(2,1)} %sg.3, bf16[2,1536,4096]{2,1,0:T(8,128)(2,1)} %su.3, ...), custom_call_target="tpu_custom_call" | custom-call | tf_op jit(solution)/shard_map/moe_0/pallas_call | solution.py:337
  73.2 14.4 %attention_1.1 = (bf16[64,1536]{1,0:T(8,128)(2,1)}, bf16[64,1664]{1,0:T(8,128)(2,1)}, f32[64,128]{1,0:T(8,128)}) custom-call(s32[64]{0:T(128)} %get-tuple-element.18.lens, bf16[64,1536]{1,0:T(8,128)(2,1)} %moe_0.1.x_ref, f32[64,128]{1,0:T(8,128)} %get-tuple-element.26.cos_ref, f32[64,128]{1,0:T(8,128)} %get-tuple-element.27.sin_ref, s32[64,2]{1,0:T(8,128)} %copy.18.ids_ref, ...), custom_call_target="tpu_custom_call" | custom-call | tf_op jit(solution)/shard_map/attention_1/pallas_call | solution.py:320
  87.6 50.1 %moe_1.1 = bf16[64,1536]{1,0:T(8,128)(2,1)} custom-call(bf16[64,1664]{1,0:T(8,128)(2,1)} %get-tuple-element.14.u_ref, bf16[64,1536]{1,0:T(8,128)(2,1)} %get-tuple-element.15.a_ref, f32[64,128]{1,0:T(8,128)} %get-tuple-element.16.meta_ref, bf16[2,1536,4096]{2,1,0:T(8,128)(2,1)} %sg.3, bf16[2,1536,4096]{2,1,0:T(8,128)(2,1)} %su.3, bf16[2,4096,1536]{2,1,0:T(8,128)(2,1)} %sd.3, ...), custom_call_target="tpu_custom_call" | custom-call | tf_op jit(solution)/shard_map/moe_1/pallas_call | solution.py:337
  137.6 1.6 %copy.20 = bf16[64,1536]{1,0:T(8,128)(2,1)} copy(bf16[64,1536]{1,0:T(8,128)(2,1)} %moe_1.1) | data formatting | bytes 393216
  (1 shorter events, 0.0 us)

commit v2 on v1

v2 whole, which is shorter than its diff:
```python
import functools
import math
import jax
import jax.numpy as jnp
from jax import lax
from jax.experimental import pallas as pl
from jax.experimental.pallas import tpu as pltpu
from jax.sharding import PartitionSpec as P

RMS_EPS = 1e-6
ROPE_BASE = 10000.0
MESH = pl.DeviceIdType.MESH
BF16 = jnp.bfloat16
F32 = jnp.float32
ANY = pl.BlockSpec(memory_space=pl.ANY)
VMEM = pl.BlockSpec(memory_space=pltpu.VMEM)
SMEM = pl.BlockSpec(memory_space=pltpu.SMEM)
VMEM_BYTES = 66_000_000
META = 128
INFO_LEN = 127
TOK_STEP = 16
FF_CHUNK = 512
LOOKAHEAD = 3
SHARED_CHUNK = 256
SHARED_RING = 4
Q_CHUNK = 256


def rms(vals):
    return vals * lax.rsqrt(jnp.mean(vals * vals, axis=-1, keepdims=True) + RMS_EPS)


def mm(lhs, rhs):
    return jnp.dot(lhs, rhs, preferred_element_type=F32)


def silu(vals):
    return vals * (1.0 / (1.0 + jnp.exp(-vals)))


def attention_kernel(layer, capacity, q_heads, kv_heads, lens, x_ref, info_ref, wr_ref, wq, wk, wv, wo, kc, vc,
                     a_ref, u_ref, meta_ref, wq_b, wk_b, wv_b, wo_b, k_b, v_b, q3, kn3, vn3, o3, attn, w_sem, q_sem, k_sem, v_sem):
    n_tok, d_model = x_ref.shape
    rows = kc.shape[2]
    head_dim = kc.shape[3]
    group = q_heads // kv_heads
    steps = n_tok // TOK_STEP
    q_steps = q_heads * head_dim // Q_CHUNK
    first = lax.axis_index("pool") * n_tok
    scale = head_dim ** -0.5
    k_copy = pltpu.make_async_copy(wk.at[layer], wk_b, w_sem.at[0])
    v_copy = pltpu.make_async_copy(wv.at[layer], wv_b, w_sem.at[1])
    o_copy = pltpu.make_async_copy(wo.at[layer], wo_b, w_sem.at[2])

    def q_copy(step):
        cols = pl.ds(step * Q_CHUNK, Q_CHUNK)
        return pltpu.make_async_copy(wq.at[layer, :, cols], wq_b.at[:, cols], q_sem.at[step])

    def cache_copies(step):
        here = pl.ds(step * TOK_STEP, TOK_STEP)
        there = pl.ds(first + step * TOK_STEP, TOK_STEP)
        return (pltpu.make_async_copy(kc.at[layer, there], k_b.at[here], k_sem.at[step]),
                pltpu.make_async_copy(vc.at[layer, there], v_b.at[here], v_sem.at[step]))

    k_copy.start()
    v_copy.start()
    for step in range(q_steps):
        q_copy(step).start()

    q3[:, q_heads:, :] = jnp.zeros((n_tok, q3.shape[1] - q_heads, head_dim), F32)
    kn3[:, q_heads:, :] = jnp.zeros((n_tok, q3.shape[1] - q_heads, head_dim), F32)
    vn3[:, q_heads:, :] = jnp.zeros((n_tok, q3.shape[1] - q_heads, head_dim), F32)
    x_f = x_ref[...].astype(F32)
    hidden = rms(x_f).astype(BF16)
    lane_d = lax.broadcasted_iota(jnp.int32, (n_tok, head_dim), 1)
    half = head_dim // 2
    inv_freq = jnp.exp(lax.rem(lane_d, half).astype(F32) * (-math.log(ROPE_BASE) / half))
    angle = info_ref[:, INFO_LEN:INFO_LEN + 1].astype(F32) * inv_freq
    cosine = jnp.cos(angle)
    sine = jnp.sin(angle)
    sine = jnp.where(lane_d < half, -sine, sine)

    def rotated(vals):
        return (vals * cosine + pltpu.roll(vals, half, 1) * sine).astype(BF16).astype(F32)

    k_copy.wait()
    key = mm(hidden, wk_b[...])
    v_copy.wait()
    val = mm(hidden, wv_b[...]).astype(BF16).astype(F32)
    for kv in range(kv_heads):
        cols = slice(kv * head_dim, (kv + 1) * head_dim)
        key_rot = rotated(key[:, cols])
        for head in range(kv * group, (kv + 1) * group):
            kn3[:, head, :] = key_rot
            vn3[:, head, :] = val[:, cols]
    started = 0
    for step in range(q_steps):
        q_copy(step).wait()
        upto = (step + 1) * steps // q_steps
        for ready in range(started, upto):
            for copy in cache_copies(ready):
                copy.start()
        started = upto
        query = mm(hidden, wq_b[:, step * Q_CHUNK:(step + 1) * Q_CHUNK])
        for i in range(Q_CHUNK // head_dim):
            q3[:, step * (Q_CHUNK // head_dim) + i, :] = rotated(query[:, i * head_dim:(i + 1) * head_dim])
    o_copy.start()

    pad = q3.shape[1]
    lane = lax.broadcasted_iota(jnp.int32, (pad, rows), 1)
    head_kv = lax.broadcasted_iota(jnp.int32, (pad, rows), 0) // group
    right_kv = lane % kv_heads == head_kv
    position = lane // kv_heads

    def step_body(step, carry):
        for copy in cache_copies(step):
            copy.wait()
        base = step * TOK_STEP
        q_f = q3[pl.ds(base, TOK_STEP)]
        scores = lax.dot_general(q_f.astype(BF16), k_b[pl.ds(base, TOK_STEP)], (((2,), (2,)), ((0,), (0,))), preferred_element_type=F32)
        s_new = jnp.sum(q_f * kn3[pl.ds(base, TOK_STEP)], axis=-1, keepdims=True) * scale
        probs = []
        p_news = []
        for i in range(TOK_STEP):
            valid = right_kv & (position < lens[first + base + i])
            s_i = jnp.where(valid, scores[i] * scale, -jnp.inf)
            peak = jnp.maximum(jnp.max(s_i, axis=-1, keepdims=True), s_new[i])
            e_i = jnp.exp(s_i - peak)
            e_new = jnp.exp(s_new[i] - peak)
            total = jnp.sum(e_i, axis=-1, keepdims=True) + e_new
            probs.append((e_i / total).astype(BF16))
            p_news.append((e_new / total).astype(BF16).astype(F32))
        for i in range(TOK_STEP):
            mixed = mm(probs[i], v_b[base + i])
            o3[base + i] = mixed + p_news[i] * vn3[base + i]
        return carry

    lax.fori_loop(0, steps, step_body, 0)
    for head in range(q_heads):
        attn[:, head * head_dim:(head + 1) * head_dim] = o3[:, head, :].astype(BF16)
    o_copy.wait()
    resid = (x_f + mm(attn[...], wo_b[...])).astype(BF16)
    a_ref[...] = resid
    normed = rms(resid.astype(F32)).astype(BF16)
    u_ref[:, :d_model] = normed

    logits = lax.dot_general(normed.astype(F32), wr_ref[layer], (((1,), (1,)), ((), ())), precision=lax.Precision.HIGHEST, preferred_element_type=F32)
    experts = logits.shape[1]
    lane_e = lax.broadcasted_iota(jnp.int32, (n_tok, META), 1)
    id0 = info_ref[:, 2 * layer:2 * layer + 1]
    id1 = info_ref[:, 2 * layer + 1:2 * layer + 2]
    pick0 = lane_e == id0
    pick1 = lane_e == id1
    l0 = jnp.sum(jnp.where(pick0[:, :experts], logits, 0.0), axis=-1, keepdims=True)
    l1 = jnp.sum(jnp.where(pick1[:, :experts], logits, 0.0), axis=-1, keepdims=True)
    peak = jnp.maximum(l0, l1)
    e0 = jnp.exp(l0 - peak)
    e1 = jnp.exp(l1 - peak)
    member = jnp.where(pick0 | pick1, 1.0, 0.0)
    earlier = jnp.where(lax.broadcasted_iota(jnp.int32, (n_tok, n_tok), 1) < lax.broadcasted_iota(jnp.int32, (n_tok, n_tok), 0), 1.0, 0.0)
    rank = mm(earlier.astype(BF16), member.astype(BF16))
    u_ref[:, d_model:] = jnp.where(member > 0.0, rank, -1.0).astype(BF16)
    slot0 = id0.astype(F32) * capacity + jnp.sum(jnp.where(pick0, rank, 0.0), axis=-1, keepdims=True)
    slot1 = id1.astype(F32) * capacity + jnp.sum(jnp.where(pick1, rank, 0.0), axis=-1, keepdims=True)
    total = e0 + e1
    meta_ref[...] = jnp.where(lane_e == 0, slot0, jnp.where(lane_e == 1, slot1, jnp.where(lane_e == 2, e0 / total, e1 / total)))


def moe_kernel(layer, capacity, ep_size, u_ref, a_ref, meta_ref, sg, su, sd, wg, wu, wd, out_ref,
               gath, back, picked, sent, acc_e, acc_s, g_w, u_w, d_w, g_b, u_b, d_b, e_sem, s_sem, ag_send, ag_recv, ret_send, ret_recv):
    n_tok = a_ref.shape[0]
    d_model = a_ref.shape[1]
    half = n_tok // 2
    e_chunks = wg.shape[3] // FF_CHUNK
    s_chunks = sg.shape[2] // SHARED_CHUNK
    me = lax.axis_index("ep")
    partner = me + 1 - 2 * lax.rem(me, 2)
    right = lax.rem(me + 2, ep_size)
    left = lax.rem(me + ep_size - 2, ep_size)
    far = lax.rem(me + ep_size // 2, ep_size)
    p_right = lax.rem(partner + 2, ep_size)
    p_left = lax.rem(partner + ep_size - 2, ep_size)
    p_far = lax.rem(partner + ep_size // 2, ep_size)
    places = [me, partner, far, p_far, right, p_right, left, p_left]

    def expert_copies(chunk):
        cols = pl.ds(chunk * FF_CHUNK, FF_CHUNK)
        pairs = ((wg.at[layer, 0, :, cols], g_w.at[:, cols]), (wu.at[layer, 0, :, cols], u_w.at[:, cols]), (wd.at[layer, 0, cols], d_w.at[cols]))
        return [pltpu.make_async_copy(src, dst, e_sem.at[chunk, i]) for i, (src, dst) in enumerate(pairs)]

    def shared_copies(chunk, slot):
        cols = pl.ds(chunk * SHARED_CHUNK, SHARED_CHUNK)
        pairs = ((sg.at[layer, :, cols], g_b.at[slot]), (su.at[layer, :, cols], u_b.at[slot]), (sd.at[layer, cols], d_b.at[slot]))
        return [pltpu.make_async_copy(src, dst, s_sem.at[slot, i]) for i, (src, dst) in enumerate(pairs)]

    for chunk in range(LOOKAHEAD):
        for copy in expert_copies(chunk):
            copy.start()

    barrier = pltpu.get_barrier_semaphore()
    for other in range(1, ep_size):
        pl.semaphore_signal(barrier, inc=1, device_id={"ep": lax.rem(me + other, ep_size)}, device_id_type=MESH)
    gath[me] = u_ref[...]
    pl.semaphore_wait(barrier, ep_size - 1)

    def piece(src, part):
        return gath.at[src, pl.ds(part * half, half)]

    def arrived(src, part):
        pltpu.make_async_remote_copy(src_ref=piece(src, part), dst_ref=piece(src, part), send_sem=ag_send.at[0], recv_sem=ag_recv.at[src, part],
                                     device_id={"ep": partner}, device_id_type=MESH).wait_recv()

    sends = []

    def send(src, part, target, from_input=False):
        ref = u_ref.at[pl.ds(part * half, half)] if from_input else piece(src, part)
        copy = pltpu.make_async_remote_copy(src_ref=ref, dst_ref=piece(src, part), send_sem=ag_send.at[len(sends)], recv_sem=ag_recv.at[src, part],
                                            device_id={"ep": target}, device_id_type=MESH)
        copy.start()
        sends.append(copy)

    send(me, 0, partner, True)
    send(me, 1, partner, True)
    send(me, 0, right, True)
    send(me, 1, left, True)
    send(me, 1, right, True)
    send(me, 0, left, True)

    acc_s[...] = jnp.zeros_like(acc_s)
    acc_e[...] = jnp.zeros_like(acc_e)
    lane = lax.broadcasted_iota(jnp.int32, (n_tok, META), 1)

    def pick(src, codes, values, place):
        rank = jnp.sum(jnp.where(lane == me, codes.astype(F32), 0.0), axis=-1, keepdims=True)
        choose = jnp.where(lane.astype(F32) == rank, 1.0, 0.0).astype(BF16)
        rows = lax.dot_general(choose, values, (((0,), (0,)), ((), ())), preferred_element_type=F32)
        picked[pl.ds(place * capacity, capacity)] = rows[:capacity].astype(BF16)

    def pick_places(first, last):
        for place in range(first, last):
            src = places[place]
            if place == 0:
                pick(src, u_ref[:, d_model:], u_ref[:, :d_model], place)
            else:
                pick(src, gath[src, :, d_model:], gath[src, :, :d_model], place)

    def expert_rows(first, last, chunk):
        rows = pl.ds(first * capacity, (last - first) * capacity)
        cols = pl.ds(pl.multiple_of(chunk * FF_CHUNK, FF_CHUNK), FF_CHUNK)
        x_rows = picked[rows]
        mid = (silu(mm(x_rows, g_w[:, cols])) * mm(x_rows, u_w[:, cols])).astype(BF16)
        acc_e[rows] += mm(mid, d_w[cols])

    def return_copy(place):
        target = places[place]
        return pltpu.make_async_remote_copy(src_ref=sent.at[place], dst_ref=back.at[me], send_sem=ret_send.at[place], recv_sem=ret_recv.at[me],
                                            device_id={"ep": target}, device_id_type=MESH)

    def give_back(first, last):
        for place in range(first, last):
            sent[place] = acc_e[pl.ds(place * capacity, capacity)].astype(BF16)
        for place in range(max(first, 1), last):
            return_copy(place).start()

    def own_step(chunk, carry):
        for copy in expert_copies(chunk):
            copy.wait()

        @pl.when(chunk + LOOKAHEAD < e_chunks)
        def _():
            for copy in expert_copies(chunk + LOOKAHEAD):
                copy.start()

        expert_rows(0, 2, chunk)
        return carry

    for part in (0, 1):
        arrived(partner, part)
    pick_places(0, 2)
    lax.fori_loop(0, 2, own_step, 0)
    arrived(left, 0)
    send(left, 0, right)
    arrived(right, 1)
    send(right, 1, left)
    send(left, 0, partner)
    send(right, 1, partner)
    lax.fori_loop(2, 4, own_step, 0)
    for src, part in ((left, 1), (right, 0)):
        arrived(src, part)
        send(src, part, partner)
    lax.fori_loop(4, 6, own_step, 0)
    for slot in range(SHARED_RING):
        for copy in shared_copies(slot, slot):
            copy.start()
    for src, part in ((far, 0), (far, 1)):
        arrived(src, part)
        send(src, part, partner)
    lax.fori_loop(6, e_chunks, own_step, 0)
    give_back(0, 2)
    for src in (p_right, p_left, p_far):
        for part in (0, 1):
            arrived(src, part)

    def full_pass(first, last):
        pick_places(first, last)

        def step(chunk, carry):
            expert_rows(first, last, chunk)
            return carry

        lax.fori_loop(0, e_chunks, step, 0)
        give_back(first, last)

    full_pass(2, 4)
    full_pass(4, 8)

    def shared_step(chunk, carry):
        slot = lax.rem(chunk, SHARED_RING)
        for copy in shared_copies(chunk, slot):
            copy.wait()
        rows = u_ref[:, :d_model]
        mid = (silu(mm(rows, g_b[slot])) * mm(rows, u_b[slot])).astype(BF16)
        acc_s[...] += mm(mid, d_b[slot])

        @pl.when(chunk + SHARED_RING < s_chunks)
        def _():
            for copy in shared_copies(chunk + SHARED_RING, slot):
                copy.start()

        return carry

    lax.fori_loop(0, s_chunks, shared_step, 0)
    back[me] = sent[0]
    for copy in sends:
        copy.wait_send()
    for place in range(1, ep_size):
        return_copy(place).wait_send()
        src = places[place]
        pltpu.make_async_remote_copy(src_ref=back.at[src], dst_ref=back.at[src], send_sem=ret_send.at[place], recv_sem=ret_recv.at[src],
                                     device_id={"ep": src}, device_id_type=MESH).wait_recv()

    slot_lane = lax.broadcasted_iota(jnp.int32, (n_tok, ep_size * capacity), 1).astype(F32)
    table = back[...].reshape(ep_size * capacity, d_model)
    y0 = mm(jnp.where(slot_lane == meta_ref[:, 0:1], 1.0, 0.0).astype(BF16), table)
    y1 = mm(jnp.where(slot_lane == meta_ref[:, 1:2], 1.0, 0.0).astype(BF16), table)
    routed = meta_ref[:, 2:3] * y0 + meta_ref[:, 3:4] * y1
    out_ref[...] = (a_ref[...].astype(F32) + routed + acc_s[...].astype(BF16).astype(F32)).astype(BF16)


def solution(mesh):
    ep_size = mesh.shape["ep"]
    row_spec = P(("dp", "ep", "pool"), None)
    cache_spec = P(None, ("dp", "ep"), None, None, None)
    expert_spec = P(None, "ep", None, None)
    in_specs = (row_spec, cache_spec, cache_spec, P(("dp", "ep")), P(), P(), P(), P(), P(), P(None, ("dp", "ep"), None), expert_spec, expert_spec, expert_spec, P(), P(), P())

    def body(x_loc, k_cache, v_cache, cache_len, w_query, w_key, w_value, w_out, w_router, expert_ids, w_gate, w_up, w_down, shared_gate, shared_up, shared_down):
        n_tok, d_model = x_loc.shape
        n_layers, all_tok, ctx, kv_heads, head_dim = k_cache.shape
        q_heads = w_query.shape[2] // head_dim
        top_k = expert_ids.shape[2]
        capacity = 3 * n_tok * top_k // ep_size
        rows = ctx * kv_heads
        pad_heads = -(-q_heads // 8) * 8
        first = lax.axis_index("pool") * n_tok
        lens = lax.dynamic_slice_in_dim(cache_len, first, n_tok, 0)
        ids = lax.dynamic_slice_in_dim(expert_ids, first, n_tok, 1)
        lane = lax.broadcasted_iota(jnp.int32, (n_tok, META), 1)
        info = jnp.where(lane == INFO_LEN, lens[:, None], 0)
        for layer in range(n_layers):
            for choice in range(top_k):
                info = jnp.where(lane == layer * top_k + choice, ids[layer, :, choice][:, None], info)
        router_t = jnp.swapaxes(w_router, 1, 2)
        k_rows = k_cache.reshape(n_layers, all_tok, rows, head_dim)
        v_rows = v_cache.reshape(n_layers, all_tok, rows, head_dim)
        ext = d_model + META
        x_cur = x_loc
        for layer in range(n_layers):
            resid, u_ext, meta = pl.pallas_call(
                functools.partial(attention_kernel, layer, capacity, q_heads, kv_heads),
                name=f"attention_{layer}",
                out_shape=(jax.ShapeDtypeStruct((n_tok, d_model), BF16), jax.ShapeDtypeStruct((n_tok, ext), BF16), jax.ShapeDtypeStruct((n_tok, META), F32)),
                in_specs=[SMEM] + [VMEM] * 3 + [ANY] * 6,
                out_specs=(VMEM, VMEM, VMEM),
                scratch_shapes=[
                    pltpu.VMEM(w_query.shape[1:], BF16), pltpu.VMEM(w_key.shape[1:], BF16), pltpu.VMEM(w_value.shape[1:], BF16), pltpu.VMEM(w_out.shape[1:], BF16),
                    pltpu.VMEM((n_tok, rows, head_dim), BF16), pltpu.VMEM((n_tok, rows, head_dim), BF16),
                    pltpu.VMEM((n_tok, pad_heads, head_dim), F32), pltpu.VMEM((n_tok, pad_heads, head_dim), F32),
                    pltpu.VMEM((n_tok, pad_heads, head_dim), F32), pltpu.VMEM((n_tok, pad_heads, head_dim), F32),
                    pltpu.VMEM((n_tok, q_heads * head_dim), BF16),
                    pltpu.SemaphoreType.DMA((3,)), pltpu.SemaphoreType.DMA((q_heads * head_dim // Q_CHUNK,)), pltpu.SemaphoreType.DMA((n_tok // TOK_STEP,)), pltpu.SemaphoreType.DMA((n_tok // TOK_STEP,)),
                ],
                compiler_params=pltpu.CompilerParams(vmem_limit_bytes=VMEM_BYTES),
            )(cache_len, x_cur, info, router_t, w_query, w_key, w_value, w_out, k_rows, v_rows)
            x_cur = pl.pallas_call(
                functools.partial(moe_kernel, layer, capacity, ep_size),
                name=f"moe_{layer}",
                out_shape=jax.ShapeDtypeStruct((n_tok, d_model), BF16),
                in_specs=[VMEM] * 3 + [ANY] * 6,
                out_specs=VMEM,
                scratch_shapes=[
                    pltpu.VMEM((ep_size, n_tok, ext), BF16), pltpu.VMEM((ep_size, capacity, d_model), BF16),
                    pltpu.VMEM((ep_size * capacity, d_model), BF16), pltpu.VMEM((ep_size, capacity, d_model), BF16),
                    pltpu.VMEM((ep_size * capacity, d_model), F32), pltpu.VMEM((n_tok, d_model), F32),
                    pltpu.VMEM(w_gate.shape[2:], BF16), pltpu.VMEM(w_up.shape[2:], BF16), pltpu.VMEM(w_down.shape[2:], BF16),
                    pltpu.VMEM((SHARED_RING, d_model, SHARED_CHUNK), BF16), pltpu.VMEM((SHARED_RING, d_model, SHARED_CHUNK), BF16), pltpu.VMEM((SHARED_RING, SHARED_CHUNK, d_model), BF16),
                    pltpu.SemaphoreType.DMA((w_gate.shape[3] // FF_CHUNK, 3)), pltpu.SemaphoreType.DMA((SHARED_RING, 3)), pltpu.SemaphoreType.DMA((14,)), pltpu.SemaphoreType.DMA((ep_size, 2)),
                    pltpu.SemaphoreType.DMA((ep_size,)), pltpu.SemaphoreType.DMA((ep_size,)),
                ],
                compiler_params=pltpu.CompilerParams(vmem_limit_bytes=VMEM_BYTES, collective_id=layer, has_side_effects=True),
            )(u_ext, resid, meta, shared_gate, shared_up, shared_down, w_gate, w_up, w_down)
        return x_cur

    return jax.shard_map(body, mesh=mesh, in_specs=in_specs, out_specs=row_spec, check_vma=False)
```

time: 140 us -> 125 us (0.89)
  Pallas kernels: 132 us -> 121 us
  local copies, waits for them, and re-layouts: 5.27 us -> 3.2 us
  other arithmetic: 2.2 us -> 0.73 us
    pallas_call x2, Pallas kernels: 103 us -> 93.2 us  [body(): pl.pallas_call(functools.partial(moe_kernel, layer, capacity, ep_size), n...]
    squeeze x4 -> x0, local copies, waits for them, and re-layouts: 3.65 us -> none  [the longest x3 2.18 us: body(): ids[layer]]
where the time goes in v2:
time: 125 us
  Pallas kernels  121 us (97%)
  local copies, waits for them, and re-layouts  3.2 us (3%)
    pallas_call x2, Pallas kernels, body(): pl.pallas_call(functools.partial(moe_kernel, layer, capacity, ep_size), n...  93.2 us
    pallas_call x2, Pallas kernels, body(): pl.pallas_call(functools.partial(attention_kernel, layer, capacity, q_hea...  27.7 us

profile of v2, /device:TPU:97, one launch (start us, length us, event | category | flops | bytes accessed | tf_op | source)
XLA Modules:
  0.0 124.8 jit_solution(2053022139490587758)
XLA Ops:
  0.0 0.8 dynamic_slice.7
  0.8 0.8 dynamic-slice_bitcast_fusion
  1.6 0.7 select_select_fusion.info_ref
  2.3 13.7 %attention_0.1 = (bf16[64,1536]{1,0:T(8,128)(2,1)}, bf16[64,1664]{1,0:T(8,128)(2,1)}, f32[64,128]{1,0:T(8,128)}) custom-call(s32[256]{0:T(256)} %lens.3, bf16[64,1536]{1,0:T(8,128)(2,1)} %x_ref.1, s32[64,128]{1,0:T(8,128)} %select_select_fusion.info_ref, f32[2,8,1536]{2,1,0:T(8,128)} %bitcast.15, bf16[2,1536,1536]{2,1,0:T(8,128)(2,1)} %wq.3, ...), custom_call_target="tpu_custom_call" | custom-call | tf_op jit(solution)/shard_map/attention_0/pallas_call | solution.py:379
  16.1 47.5 %moe_0.1.x_ref = bf16[64,1536]{1,0:T(8,128)(2,1)} custom-call(bf16[64,1664]{1,0:T(8,128)(2,1)} %get-tuple-element.11.u_ref, bf16[64,1536]{1,0:T(8,128)(2,1)} %get-tuple-element.12.a_ref, f32[64,128]{1,0:T(8,128)} %get-tuple-element.13.meta_ref, bf16[2,1536,4096]{2,1,0:T(8,128)(2,1)} %sg.3, bf16[2,1536,4096]{2,1,0:T(8,128)(2,1)} %su.3, ...), custom_call_target="tpu_custom_call" | custom-call | tf_op jit(solution)/shard_map/moe_0/pallas_call | solution.py:395
  63.6 13.9 %attention_1.1 = (bf16[64,1536]{1,0:T(8,128)(2,1)}, bf16[64,1664]{1,0:T(8,128)(2,1)}, f32[64,128]{1,0:T(8,128)}) custom-call(s32[256]{0:T(256)} %lens.3, bf16[64,1536]{1,0:T(8,128)(2,1)} %moe_0.1.x_ref, s32[64,128]{1,0:T(8,128)} %select_select_fusion.info_ref, f32[2,8,1536]{2,1,0:T(8,128)} %bitcast.16, bf16[2,1536,1536]{2,1,0:T(8,128)(2,1)} %wq.3, ...), custom_call_target="tpu_custom_call" | custom-call | tf_op jit(solution)/shard_map/attention_1/pallas_call | solution.py:379
  77.5 45.6 %moe_1.1 = bf16[64,1536]{1,0:T(8,128)(2,1)} custom-call(bf16[64,1664]{1,0:T(8,128)(2,1)} %get-tuple-element.14.u_ref, bf16[64,1536]{1,0:T(8,128)(2,1)} %get-tuple-element.15.a_ref, f32[64,128]{1,0:T(8,128)} %get-tuple-element.16.meta_ref, bf16[2,1536,4096]{2,1,0:T(8,128)(2,1)} %sg.3, bf16[2,1536,4096]{2,1,0:T(8,128)(2,1)} %su.3, bf16[2,4096,1536]{2,1,0:T(8,128)(2,1)} %sd.3, ...), custom_call_target="tpu_custom_call" | custom-call | tf_op jit(solution)/shard_map/moe_1/pallas_call | solution.py:395
  123.2 1.6 %copy.18 = bf16[64,1536]{1,0:T(8,128)(2,1)} copy(bf16[64,1536]{1,0:T(8,128)(2,1)} %moe_1.1) | data formatting | bytes 393216
  (3 shorter events, 0.0 us)

commit v3 on v2

--- a/solution.py
+++ b/solution.py
@@ -21,9 +21,12 @@
 TOK_STEP = 16
 FF_CHUNK = 512
 LOOKAHEAD = 3
-SHARED_CHUNK = 256
-SHARED_RING = 4
-Q_CHUNK = 256
+PASS_CHUNK = 2048
+SHARED_CHUNK = 512
+SHARED_RING = 2
+Q_CHUNK = 512
+CHIP_CORES = 2
+ROW_TILE = 128
 
 
 def rms(vals):
@@ -62,10 +65,13 @@
         return (pltpu.make_async_copy(kc.at[layer, there], k_b.at[here], k_sem.at[step]),
                 pltpu.make_async_copy(vc.at[layer, there], v_b.at[here], v_sem.at[step]))
 
+    def start_cache(step):
+        for copy in cache_copies(step):
+            copy.start()
+
     k_copy.start()
     v_copy.start()
-    for step in range(q_steps):
-        q_copy(step).start()
+    q_copy(0).start()
 
     q3[:, q_heads:, :] = jnp.zeros((n_tok, q3.shape[1] - q_heads, head_dim), F32)
     kn3[:, q_heads:, :] = jnp.zeros((n_tok, q3.shape[1] - q_heads, head_dim), F32)
@@ -84,8 +90,10 @@
         return (vals * cosine + pltpu.roll(vals, half, 1) * sine).astype(BF16).astype(F32)
 
     k_copy.wait()
+    q_copy(1).start()
     key = mm(hidden, wk_b[...])
     v_copy.wait()
+    q_copy(2).start()
     val = mm(hidden, wv_b[...]).astype(BF16).astype(F32)
     for kv in range(kv_heads):
         cols = slice(kv * head_dim, (kv + 1) * head_dim)
@@ -93,17 +101,14 @@
         for head in range(kv * group, (kv + 1) * group):
             kn3[:, head, :] = key_rot
             vn3[:, head, :] = val[:, cols]
-    started = 0
     for step in range(q_steps):
         q_copy(step).wait()
-        upto = (step + 1) * steps // q_steps
-        for ready in range(started, upto):
-            for copy in cache_copies(ready):
-                copy.start()
-        started = upto
+        start_cache(step)
         query = mm(hidden, wq_b[:, step * Q_CHUNK:(step + 1) * Q_CHUNK])
         for i in range(Q_CHUNK // head_dim):
             q3[:, step * (Q_CHUNK // head_dim) + i, :] = rotated(query[:, i * head_dim:(i + 1) * head_dim])
+    for step in range(q_steps, steps):
+        start_cache(step)
     o_copy.start()
 
     pad = q3.shape[1]
@@ -166,13 +171,18 @@
     meta_ref[...] = jnp.where(lane_e == 0, slot0, jnp.where(lane_e == 1, slot1, jnp.where(lane_e == 2, e0 / total, e1 / total)))
 
 
+def row_blocks(capacity, blocks=((0, 2), (2, 4), (4, 8))):
+    sizes = [-(-(hi - lo) * capacity // ROW_TILE) * ROW_TILE if (hi - lo) * capacity < ROW_TILE else (hi - lo) * capacity for lo, hi in blocks]
+    return [sum(sizes[:i]) for i in range(len(sizes))], sizes
+
+
 def moe_kernel(layer, capacity, ep_size, u_ref, a_ref, meta_ref, sg, su, sd, wg, wu, wd, out_ref,
-               gath, back, picked, sent, acc_e, acc_s, g_w, u_w, d_w, g_b, u_b, d_b, e_sem, s_sem, ag_send, ag_recv, ret_send, ret_recv):
+               gath, back, picked, sent, acc_e, acc_s, pair, other_s, g_w, u_w, d_w, g_b, u_b, d_b, e_sem, s_sem, ag_send, ag_recv, ret_send, ret_recv, sum_send, sum_recv):
     n_tok = a_ref.shape[0]
     d_model = a_ref.shape[1]
     half = n_tok // 2
     e_chunks = wg.shape[3] // FF_CHUNK
-    s_chunks = sg.shape[2] // SHARED_CHUNK
+    s_chunks = sg.shape[2] // (SHARED_CHUNK * CHIP_CORES)
     me = lax.axis_index("ep")
     partner = me + 1 - 2 * lax.rem(me, 2)
     right = lax.rem(me + 2, ep_size)
@@ -182,14 +192,19 @@
     p_left = lax.rem(partner + ep_size - 2, ep_size)
     p_far = lax.rem(partner + ep_size // 2, ep_size)
     places = [me, partner, far, p_far, right, p_right, left, p_left]
+    blocks = [(0, 2), (2, 4), (4, 8)]
+    starts, sizes = row_blocks(capacity, blocks)
+    row_of = {place: starts[i] + (place - lo) * capacity for i, (lo, hi) in enumerate(blocks) for place in range(lo, hi)}
 
     def expert_copies(chunk):
         cols = pl.ds(chunk * FF_CHUNK, FF_CHUNK)
         pairs = ((wg.at[layer, 0, :, cols], g_w.at[:, cols]), (wu.at[layer, 0, :, cols], u_w.at[:, cols]), (wd.at[layer, 0, cols], d_w.at[cols]))
         return [pltpu.make_async_copy(src, dst, e_sem.at[chunk, i]) for i, (src, dst) in enumerate(pairs)]
 
+    s_first = lax.rem(me, CHIP_CORES) * s_chunks
+
     def shared_copies(chunk, slot):
-        cols = pl.ds(chunk * SHARED_CHUNK, SHARED_CHUNK)
+        cols = pl.ds((s_first + chunk) * SHARED_CHUNK, SHARED_CHUNK)
         pairs = ((sg.at[layer, :, cols], g_b.at[slot]), (su.at[layer, :, cols], u_b.at[slot]), (sd.at[layer, cols], d_b.at[slot]))
         return [pltpu.make_async_copy(src, dst, s_sem.at[slot, i]) for i, (src, dst) in enumerate(pairs)]
 
@@ -228,13 +243,14 @@
 
     acc_s[...] = jnp.zeros_like(acc_s)
     acc_e[...] = jnp.zeros_like(acc_e)
+    picked[...] = jnp.zeros_like(picked)
     lane = lax.broadcasted_iota(jnp.int32, (n_tok, META), 1)
 
     def pick(src, codes, values, place):
         rank = jnp.sum(jnp.where(lane == me, codes.astype(F32), 0.0), axis=-1, keepdims=True)
         choose = jnp.where(lane.astype(F32) == rank, 1.0, 0.0).astype(BF16)
         rows = lax.dot_general(choose, values, (((0,), (0,)), ((), ())), preferred_element_type=F32)
-        picked[pl.ds(place * capacity, capacity)] = rows[:capacity].astype(BF16)
+        picked[pl.ds(row_of[place], capacity)] = rows[:capacity].astype(BF16)
 
     def pick_places(first, last):
         for place in range(first, last):
@@ -244,9 +260,9 @@
             else:
                 pick(src, gath[src, :, d_model:], gath[src, :, :d_model], place)
 
-    def expert_rows(first, last, chunk):
-        rows = pl.ds(first * capacity, (last - first) * capacity)
-        cols = pl.ds(pl.multiple_of(chunk * FF_CHUNK, FF_CHUNK), FF_CHUNK)
+    def expert_rows(block, chunk, width):
+        rows = pl.ds(starts[block], sizes[block])
+        cols = pl.ds(pl.multiple_of(chunk * width, width), width)
         x_rows = picked[rows]
         mid = (silu(mm(x_rows, g_w[:, cols])) * mm(x_rows, u_w[:, cols])).astype(BF16)
         acc_e[rows] += mm(mid, d_w[cols])
@@ -258,7 +274,7 @@
 
     def give_back(first, last):
         for place in range(first, last):
-            sent[place] = acc_e[pl.ds(place * capacity, capacity)].astype(BF16)
+            sent[place] = acc_e[pl.ds(row_of[place], capacity)].astype(BF16)
         for place in range(max(first, 1), last):
             return_copy(place).start()
 
@@ -271,7 +287,7 @@
             for copy in expert_copies(chunk + LOOKAHEAD):
                 copy.start()
 
-        expert_rows(0, 2, chunk)
+        expert_rows(0, chunk, FF_CHUNK)
         return carry
 
     for part in (0, 1):
@@ -301,24 +317,27 @@
         for part in (0, 1):
             arrived(src, part)
 
-    def full_pass(first, last):
+    def full_pass(block):
+        first, last = blocks[block]
         pick_places(first, last)
 
         def step(chunk, carry):
-            expert_rows(first, last, chunk)
+            expert_rows(block, chunk, PASS_CHUNK)
             return carry
 
-        lax.fori_loop(0, e_chunks, step, 0)
+        lax.fori_loop(0, wg.shape[3] // PASS_CHUNK, step, 0)
         give_back(first, last)
 
-    full_pass(2, 4)
-    full_pass(4, 8)
+    full_pass(1)
+    full_pass(2)
+    pair[pl.ds(0, n_tok)] = u_ref[:, :d_model]
+    pair[pl.ds(n_tok, n_tok)] = gath[partner, :, :d_model]
 
     def shared_step(chunk, carry):
         slot = lax.rem(chunk, SHARED_RING)
         for copy in shared_copies(chunk, slot):
             copy.wait()
-        rows = u_ref[:, :d_model]
+        rows = pair[...]
         mid = (silu(mm(rows, g_b[slot])) * mm(rows, u_b[slot])).astype(BF16)
         acc_s[...] += mm(mid, d_b[slot])
 
@@ -330,6 +349,9 @@
         return carry
 
     lax.fori_loop(0, s_chunks, shared_step, 0)
+    sum_copy = pltpu.make_async_remote_copy(src_ref=acc_s.at[pl.ds(n_tok, n_tok)], dst_ref=other_s, send_sem=sum_send, recv_sem=sum_recv,
+                                            device_id={"ep": partner}, device_id_type=MESH)
+    sum_copy.start()
     back[me] = sent[0]
     for copy in sends:
         copy.wait_send()
@@ -341,10 +363,12 @@
 
     slot_lane = lax.broadcasted_iota(jnp.int32, (n_tok, ep_size * capacity), 1).astype(F32)
     table = back[...].reshape(ep_size * capacity, d_model)
-    y0 = mm(jnp.where(slot_lane == meta_ref[:, 0:1], 1.0, 0.0).astype(BF16), table)
-    y1 = mm(jnp.where(slot_lane == meta_ref[:, 1:2], 1.0, 0.0).astype(BF16), table)
-    routed = meta_ref[:, 2:3] * y0 + meta_ref[:, 3:4] * y1
-    out_ref[...] = (a_ref[...].astype(F32) + routed + acc_s[...].astype(BF16).astype(F32)).astype(BF16)
+    choose = jnp.concatenate([jnp.where(slot_lane == meta_ref[:, 0:1], 1.0, 0.0), jnp.where(slot_lane == meta_ref[:, 1:2], 1.0, 0.0)], axis=0).astype(BF16)
+    y_pair = mm(choose, table)
+    routed = meta_ref[:, 2:3] * y_pair[:n_tok] + meta_ref[:, 3:4] * y_pair[n_tok:]
+    sum_copy.wait()
+    shared_out = (acc_s[pl.ds(0, n_tok)] + other_s[...]).astype(BF16).astype(F32)
+    out_ref[...] = (a_ref[...].astype(F32) + routed + shared_out).astype(BF16)
 
 
 def solution(mesh):
@@ -374,6 +398,7 @@
         k_rows = k_cache.reshape(n_layers, all_tok, rows, head_dim)
         v_rows = v_cache.reshape(n_layers, all_tok, rows, head_dim)
         ext = d_model + META
+        n_rows = sum(row_blocks(capacity)[1])
         x_cur = x_loc
         for layer in range(n_layers):
             resid, u_ext, meta = pl.pallas_call(
@@ -400,12 +425,13 @@
                 out_specs=VMEM,
                 scratch_shapes=[
                     pltpu.VMEM((ep_size, n_tok, ext), BF16), pltpu.VMEM((ep_size, capacity, d_model), BF16),
-                    pltpu.VMEM((ep_size * capacity, d_model), BF16), pltpu.VMEM((ep_size, capacity, d_model), BF16),
-                    pltpu.VMEM((ep_size * capacity, d_model), F32), pltpu.VMEM((n_tok, d_model), F32),
+                    pltpu.VMEM((n_rows, d_model), BF16), pltpu.VMEM((ep_size, capacity, d_model), BF16),
+                    pltpu.VMEM((n_rows, d_model), F32), pltpu.VMEM((CHIP_CORES * n_tok, d_model), F32),
+                    pltpu.VMEM((CHIP_CORES * n_tok, d_model), BF16), pltpu.VMEM((n_tok, d_model), F32),
                     pltpu.VMEM(w_gate.shape[2:], BF16), pltpu.VMEM(w_up.shape[2:], BF16), pltpu.VMEM(w_down.shape[2:], BF16),
                     pltpu.VMEM((SHARED_RING, d_model, SHARED_CHUNK), BF16), pltpu.VMEM((SHARED_RING, d_model, SHARED_CHUNK), BF16), pltpu.VMEM((SHARED_RING, SHARED_CHUNK, d_model), BF16),
                     pltpu.SemaphoreType.DMA((w_gate.shape[3] // FF_CHUNK, 3)), pltpu.SemaphoreType.DMA((SHARED_RING, 3)), pltpu.SemaphoreType.DMA((14,)), pltpu.SemaphoreType.DMA((ep_size, 2)),
-                    pltpu.SemaphoreType.DMA((ep_size,)), pltpu.SemaphoreType.DMA((ep_size,)),
+                    pltpu.SemaphoreType.DMA((ep_size,)), pltpu.SemaphoreType.DMA((ep_size,)), pltpu.SemaphoreType.DMA, pltpu.SemaphoreType.DMA,
                 ],
                 compiler_params=pltpu.CompilerParams(vmem_limit_bytes=VMEM_BYTES, collective_id=layer, has_side_effects=True),
             )(u_ext, resid, meta, shared_gate, shared_up, shared_down, w_gate, w_up, w_down)

time: 125 us -> 109 us (0.87)
  Pallas kernels: 121 us -> 105 us
    pallas_call x2, Pallas kernels: 93.2 us -> 80.2 us  [body(): pl.pallas_call(functools.partial(moe_kernel, layer, capacity, ep_size), n...]
    pallas_call x2, Pallas kernels: 27.7 us -> 24.9 us  [body(): pl.pallas_call(functools.partial(attention_kernel, layer, capacity, q_hea...]
where the time goes in v3:
time: 109 us
  Pallas kernels  105 us (96%)
  local copies, waits for them, and re-layouts  3.2 us (3%)
    pallas_call x2, Pallas kernels, body(): pl.pallas_call(functools.partial(moe_kernel, layer, capacity, ep_size), n...  80.2 us
    pallas_call x2, Pallas kernels, body(): pl.pallas_call(functools.partial(attention_kernel, layer, capacity, q_hea...  24.9 us

profile of v3, /device:TPU:97, one launch (start us, length us, event | category | flops | bytes accessed | tf_op | source)
XLA Modules:
  0.0 109.0 jit_solution(6845127912576459110)
XLA Ops:
  0.0 0.8 dynamic_slice.7
  0.8 0.8 dynamic-slice_bitcast_fusion
  1.6 0.7 select_select_fusion.info_ref
  2.3 12.4 %attention_0.1 = (bf16[64,1536]{1,0:T(8,128)(2,1)}, bf16[64,1664]{1,0:T(8,128)(2,1)}, f32[64,128]{1,0:T(8,128)}) custom-call(s32[256]{0:T(256)} %lens.3, bf16[64,1536]{1,0:T(8,128)(2,1)} %x_ref.1, s32[64,128]{1,0:T(8,128)} %select_select_fusion.info_ref, f32[2,8,1536]{2,1,0:T(8,128)} %bitcast.15, bf16[2,1536,1536]{2,1,0:T(8,128)(2,1)} %wq.3, ...), custom_call_target="tpu_custom_call" | custom-call | tf_op jit(solution)/shard_map/attention_0/pallas_call | solution.py:404
  14.8 41.5 %moe_0.1.x_ref = bf16[64,1536]{1,0:T(8,128)(2,1)} custom-call(bf16[64,1664]{1,0:T(8,128)(2,1)} %get-tuple-element.11.u_ref, bf16[64,1536]{1,0:T(8,128)(2,1)} %get-tuple-element.12.a_ref, f32[64,128]{1,0:T(8,128)} %get-tuple-element.13.meta_ref, bf16[2,1536,4096]{2,1,0:T(8,128)(2,1)} %sg.3, bf16[2,1536,4096]{2,1,0:T(8,128)(2,1)} %su.3, ...), custom_call_target="tpu_custom_call" | custom-call | tf_op jit(solution)/shard_map/moe_0/pallas_call | solution.py:420
  56.2 12.4 %attention_1.1 = (bf16[64,1536]{1,0:T(8,128)(2,1)}, bf16[64,1664]{1,0:T(8,128)(2,1)}, f32[64,128]{1,0:T(8,128)}) custom-call(s32[256]{0:T(256)} %lens.3, bf16[64,1536]{1,0:T(8,128)(2,1)} %moe_0.1.x_ref, s32[64,128]{1,0:T(8,128)} %select_select_fusion.info_ref, f32[2,8,1536]{2,1,0:T(8,128)} %bitcast.16, bf16[2,1536,1536]{2,1,0:T(8,128)(2,1)} %wq.3, ...), custom_call_target="tpu_custom_call" | custom-call | tf_op jit(solution)/shard_map/attention_1/pallas_call | solution.py:404
  68.7 38.7 %moe_1.1 = bf16[64,1536]{1,0:T(8,128)(2,1)} custom-call(bf16[64,1664]{1,0:T(8,128)(2,1)} %get-tuple-element.14.u_ref, bf16[64,1536]{1,0:T(8,128)(2,1)} %get-tuple-element.15.a_ref, f32[64,128]{1,0:T(8,128)} %get-tuple-element.16.meta_ref, bf16[2,1536,4096]{2,1,0:T(8,128)(2,1)} %sg.3, bf16[2,1536,4096]{2,1,0:T(8,128)(2,1)} %su.3, bf16[2,4096,1536]{2,1,0:T(8,128)(2,1)} %sd.3, ...), custom_call_target="tpu_custom_call" | custom-call | tf_op jit(solution)/shard_map/moe_1/pallas_call | solution.py:420
  107.4 1.6 %copy.18 = bf16[64,1536]{1,0:T(8,128)(2,1)} copy(bf16[64,1536]{1,0:T(8,128)(2,1)} %moe_1.1) | data formatting | bytes 393216
  (3 shorter events, 0.0 us)

commit v4 on v3

--- a/solution.py
+++ b/solution.py
@@ -17,10 +17,10 @@
 SMEM = pl.BlockSpec(memory_space=pltpu.SMEM)
 VMEM_BYTES = 66_000_000
 META = 128
-INFO_LEN = 127
 TOK_STEP = 16
 FF_CHUNK = 512
 LOOKAHEAD = 3
+OWN_FIRST = 5
 PASS_CHUNK = 2048
 SHARED_CHUNK = 512
 SHARED_RING = 2
@@ -41,7 +41,7 @@
     return vals * (1.0 / (1.0 + jnp.exp(-vals)))
 
 
-def attention_kernel(layer, capacity, q_heads, kv_heads, lens, x_ref, info_ref, wr_ref, wq, wk, wv, wo, kc, vc,
+def attention_kernel(layer, capacity, q_heads, kv_heads, lens, x_ref, row_len_ref, ids_ref, wr_ref, wq, wk, wv, wo, kc, vc,
                      a_ref, u_ref, meta_ref, wq_b, wk_b, wv_b, wo_b, k_b, v_b, q3, kn3, vn3, o3, attn, w_sem, q_sem, k_sem, v_sem):
     n_tok, d_model = x_ref.shape
     rows = kc.shape[2]
@@ -76,12 +76,18 @@
     q3[:, q_heads:, :] = jnp.zeros((n_tok, q3.shape[1] - q_heads, head_dim), F32)
     kn3[:, q_heads:, :] = jnp.zeros((n_tok, q3.shape[1] - q_heads, head_dim), F32)
     vn3[:, q_heads:, :] = jnp.zeros((n_tok, q3.shape[1] - q_heads, head_dim), F32)
+    all_tok = row_len_ref.shape[1]
+    mine = lax.broadcasted_iota(jnp.int32, (n_tok, all_tok), 1) == first + lax.broadcasted_iota(jnp.int32, (n_tok, all_tok), 0)
+
+    def column(row):
+        return jnp.sum(jnp.where(mine, row.astype(F32), 0.0), axis=-1, keepdims=True)
+
     x_f = x_ref[...].astype(F32)
     hidden = rms(x_f).astype(BF16)
     lane_d = lax.broadcasted_iota(jnp.int32, (n_tok, head_dim), 1)
     half = head_dim // 2
     inv_freq = jnp.exp(lax.rem(lane_d, half).astype(F32) * (-math.log(ROPE_BASE) / half))
-    angle = info_ref[:, INFO_LEN:INFO_LEN + 1].astype(F32) * inv_freq
+    angle = column(row_len_ref[...]) * inv_freq
     cosine = jnp.cos(angle)
     sine = jnp.sin(angle)
     sine = jnp.where(lane_d < half, -sine, sine)
@@ -151,9 +157,9 @@
 
     logits = lax.dot_general(normed.astype(F32), wr_ref[layer], (((1,), (1,)), ((), ())), precision=lax.Precision.HIGHEST, preferred_element_type=F32)
     experts = logits.shape[1]
-    lane_e = lax.broadcasted_iota(jnp.int32, (n_tok, META), 1)
-    id0 = info_ref[:, 2 * layer:2 * layer + 1]
-    id1 = info_ref[:, 2 * layer + 1:2 * layer + 2]
+    lane_e = lax.broadcasted_iota(jnp.int32, (n_tok, META), 1).astype(F32)
+    id0 = column(ids_ref[layer, 0:1, :])
+    id1 = column(ids_ref[layer, 1:2, :])
     pick0 = lane_e == id0
     pick1 = lane_e == id1
     l0 = jnp.sum(jnp.where(pick0[:, :experts], logits, 0.0), axis=-1, keepdims=True)
@@ -165,8 +171,8 @@
     earlier = jnp.where(lax.broadcasted_iota(jnp.int32, (n_tok, n_tok), 1) < lax.broadcasted_iota(jnp.int32, (n_tok, n_tok), 0), 1.0, 0.0)
     rank = mm(earlier.astype(BF16), member.astype(BF16))
     u_ref[:, d_model:] = jnp.where(member > 0.0, rank, -1.0).astype(BF16)
-    slot0 = id0.astype(F32) * capacity + jnp.sum(jnp.where(pick0, rank, 0.0), axis=-1, keepdims=True)
-    slot1 = id1.astype(F32) * capacity + jnp.sum(jnp.where(pick1, rank, 0.0), axis=-1, keepdims=True)
+    slot0 = id0 * capacity + jnp.sum(jnp.where(pick0, rank, 0.0), axis=-1, keepdims=True)
+    slot1 = id1 * capacity + jnp.sum(jnp.where(pick1, rank, 0.0), axis=-1, keepdims=True)
     total = e0 + e1
     meta_ref[...] = jnp.where(lane_e == 0, slot0, jnp.where(lane_e == 1, slot1, jnp.where(lane_e == 2, e0 / total, e1 / total)))
 
@@ -304,32 +310,60 @@
     for src, part in ((left, 1), (right, 0)):
         arrived(src, part)
         send(src, part, partner)
-    lax.fori_loop(4, 6, own_step, 0)
+    lax.fori_loop(4, OWN_FIRST, own_step, 0)
     for slot in range(SHARED_RING):
         for copy in shared_copies(slot, slot):
             copy.start()
-    for src, part in ((far, 0), (far, 1)):
-        arrived(src, part)
-        send(src, part, partner)
-    lax.fori_loop(6, e_chunks, own_step, 0)
-    give_back(0, 2)
-    for src in (p_right, p_left, p_far):
+    for src in (p_right, p_left):
         for part in (0, 1):
             arrived(src, part)
-
-    def full_pass(block):
-        first, last = blocks[block]
-        pick_places(first, last)
-
-        def step(chunk, carry):
-            expert_rows(block, chunk, PASS_CHUNK)
-            return carry
-
-        lax.fori_loop(0, wg.shape[3] // PASS_CHUNK, step, 0)
-        give_back(first, last)
-
-    full_pass(1)
-    full_pass(2)
+    pick_places(4, 8)
+    per_step = PASS_CHUNK // FF_CHUNK
+    sent_before = len(sends)
+
+    def far_copy(part):
+        return pltpu.make_async_remote_copy(src_ref=piece(far, part), dst_ref=piece(far, part), send_sem=ag_send.at[sent_before + part],
+                                            recv_sem=ag_recv.at[far, part], device_id={"ep": partner}, device_id_type=MESH)
+
+
+    def near_step(step, carry):
+        for chunk in range(OWN_FIRST, e_chunks):
+
+            @pl.when(step == chunk // per_step)
+            def _():
+                for copy in expert_copies(chunk):
+                    copy.wait()
+
+        expert_rows(2, step, PASS_CHUNK)
+
+        @pl.when(step == 0)
+        def _():
+            for part in (0, 1):
+                arrived(far, part)
+                far_copy(part).start()
+
+        return carry
+
+    lax.fori_loop(0, e_chunks // per_step, near_step, 0)
+    give_back(4, 8)
+    for src in (p_far,):
+        for part in (0, 1):
+            arrived(src, part)
+    pick_places(2, 4)
+
+    def far_step(step, carry):
+        expert_rows(1, step, PASS_CHUNK)
+        return carry
+
+    lax.fori_loop(0, e_chunks // per_step, far_step, 0)
+    give_back(2, 4)
+
+    def own_rest(chunk, carry):
+        expert_rows(0, chunk, FF_CHUNK)
+        return carry
+
+    lax.fori_loop(OWN_FIRST, e_chunks, own_rest, 0)
+    give_back(0, 2)
     pair[pl.ds(0, n_tok)] = u_ref[:, :d_model]
     pair[pl.ds(n_tok, n_tok)] = gath[partner, :, :d_model]
 
@@ -353,7 +387,7 @@
                                             device_id={"ep": partner}, device_id_type=MESH)
     sum_copy.start()
     back[me] = sent[0]
-    for copy in sends:
+    for copy in sends + [far_copy(0), far_copy(1)]:
         copy.wait_send()
     for place in range(1, ep_size):
         return_copy(place).wait_send()
@@ -386,14 +420,8 @@
         capacity = 3 * n_tok * top_k // ep_size
         rows = ctx * kv_heads
         pad_heads = -(-q_heads // 8) * 8
-        first = lax.axis_index("pool") * n_tok
-        lens = lax.dynamic_slice_in_dim(cache_len, first, n_tok, 0)
-        ids = lax.dynamic_slice_in_dim(expert_ids, first, n_tok, 1)
-        lane = lax.broadcasted_iota(jnp.int32, (n_tok, META), 1)
-        info = jnp.where(lane == INFO_LEN, lens[:, None], 0)
-        for layer in range(n_layers):
-            for choice in range(top_k):
-                info = jnp.where(lane == layer * top_k + choice, ids[layer, :, choice][:, None], info)
+        ids_t = jnp.swapaxes(expert_ids, 1, 2)
+        row_len = cache_len.reshape(1, cache_len.shape[0])
         router_t = jnp.swapaxes(w_router, 1, 2)
         k_rows = k_cache.reshape(n_layers, all_tok, rows, head_dim)
         v_rows = v_cache.reshape(n_layers, all_tok, rows, head_dim)
@@ -405,7 +433,7 @@
                 functools.partial(attention_kernel, layer, capacity, q_heads, kv_heads),
                 name=f"attention_{layer}",
                 out_shape=(jax.ShapeDtypeStruct((n_tok, d_model), BF16), jax.ShapeDtypeStruct((n_tok, ext), BF16), jax.ShapeDtypeStruct((n_tok, META), F32)),
-                in_specs=[SMEM] + [VMEM] * 3 + [ANY] * 6,
+                in_specs=[SMEM] + [VMEM] * 4 + [ANY] * 6,
                 out_specs=(VMEM, VMEM, VMEM),
                 scratch_shapes=[
                     pltpu.VMEM(w_query.shape[1:], BF16), pltpu.VMEM(w_key.shape[1:], BF16), pltpu.VMEM(w_value.shape[1:], BF16), pltpu.VMEM(w_out.shape[1:], BF16),
@@ -416,7 +444,7 @@
                     pltpu.SemaphoreType.DMA((3,)), pltpu.SemaphoreType.DMA((q_heads * head_dim // Q_CHUNK,)), pltpu.SemaphoreType.DMA((n_tok // TOK_STEP,)), pltpu.SemaphoreType.DMA((n_tok // TOK_STEP,)),
                 ],
                 compiler_params=pltpu.CompilerParams(vmem_limit_bytes=VMEM_BYTES),
-            )(cache_len, x_cur, info, router_t, w_query, w_key, w_value, w_out, k_rows, v_rows)
+            )(cache_len, x_cur, row_len, ids_t, router_t, w_query, w_key, w_value, w_out, k_rows, v_rows)
             x_cur = pl.pallas_call(
                 functools.partial(moe_kernel, layer, capacity, ep_size),
                 name=f"moe_{layer}",

time: 109 us -> 104 us (0.954)
  Pallas kernels: 105 us -> 102 us
  local copies, waits for them, and re-layouts: 3.2 us -> 1.62 us
    pallas_call x2, Pallas kernels: 80.2 us -> 77 us  [body(): pl.pallas_call(functools.partial(moe_kernel, layer, capacity, ep_size), n...]
where the time goes in v4:
time: 104 us; the launch traced here: 103 us
  Pallas kernels  102 us (98%)
  local copies, waits for them, and re-layouts  1.62 us (2%)
    pallas_call x2, Pallas kernels, body(): pl.pallas_call(functools.partial(moe_kernel, layer, capacity, ep_size), n...  77 us
    pallas_call x2, Pallas kernels, body(): pl.pallas_call(functools.partial(attention_kernel, layer, capacity, q_hea...  24.8 us

profile of v4, /device:TPU:97, one launch (start us, length us, event | category | flops | bytes accessed | tf_op | source)
XLA Modules:
  0.0 103.4 jit_solution(4808001415825102103)
XLA Ops:
  0.0 12.4 %attention_0.1 = (bf16[64,1536]{1,0:T(8,128)(2,1)}, bf16[64,1664]{1,0:T(8,128)(2,1)}, f32[64,128]{1,0:T(8,128)}) custom-call(s32[256]{0:T(256)} %lens.3, bf16[64,1536]{1,0:T(8,128)(2,1)} %x_ref.1, s32[1,256]{1,0:T(1,128)} %bitcast.13, s32[2,2,256]{2,1,0:T(2,128)} %bitcast.11, f32[2,8,1536]{2,1,0:T(8,128)} %bitcast.9, bf16[2,1536,1536]{2,1,0:T(8,128)(2,1)} %wq.3, ...), custom_call_target="tpu_custom_call" | custom-call | tf_op jit(solution)/shard_map/attention_0/pallas_call | solution.py:432
  12.4 39.6 %moe_0.1.x_ref = bf16[64,1536]{1,0:T(8,128)(2,1)} custom-call(bf16[64,1664]{1,0:T(8,128)(2,1)} %get-tuple-element.11.u_ref, bf16[64,1536]{1,0:T(8,128)(2,1)} %get-tuple-element.12.a_ref, f32[64,128]{1,0:T(8,128)} %get-tuple-element.13.meta_ref, bf16[2,1536,4096]{2,1,0:T(8,128)(2,1)} %sg.3, bf16[2,1536,4096]{2,1,0:T(8,128)(2,1)} %su.3, ...), custom_call_target="tpu_custom_call" | custom-call | tf_op jit(solution)/shard_map/moe_0/pallas_call | solution.py:448
  52.0 12.4 %attention_1.1 = (bf16[64,1536]{1,0:T(8,128)(2,1)}, bf16[64,1664]{1,0:T(8,128)(2,1)}, f32[64,128]{1,0:T(8,128)}) custom-call(s32[256]{0:T(256)} %lens.3, bf16[64,1536]{1,0:T(8,128)(2,1)} %moe_0.1.x_ref, s32[1,256]{1,0:T(1,128)} %bitcast.14, s32[2,2,256]{2,1,0:T(2,128)} %bitcast.12, f32[2,8,1536]{2,1,0:T(8,128)} %bitcast.10, bf16[2,1536,1536]{2,1,0:T(8,128)(2,1)} %wq.3, ...), custom_call_target="tpu_custom_call" | custom-call | tf_op jit(solution)/shard_map/attention_1/pallas_call | solution.py:432
  64.4 37.4 %moe_1.1 = bf16[64,1536]{1,0:T(8,128)(2,1)} custom-call(bf16[64,1664]{1,0:T(8,128)(2,1)} %get-tuple-element.14.u_ref, bf16[64,1536]{1,0:T(8,128)(2,1)} %get-tuple-element.15.a_ref, f32[64,128]{1,0:T(8,128)} %get-tuple-element.16.meta_ref, bf16[2,1536,4096]{2,1,0:T(8,128)(2,1)} %sg.3, bf16[2,1536,4096]{2,1,0:T(8,128)(2,1)} %su.3, bf16[2,4096,1536]{2,1,0:T(8,128)(2,1)} %sd.3, ...), custom_call_target="tpu_custom_call" | custom-call | tf_op jit(solution)/shard_map/moe_1/pallas_call | solution.py:448
  101.8 1.6 %copy.18 = bf16[64,1536]{1,0:T(8,128)(2,1)} copy(bf16[64,1536]{1,0:T(8,128)(2,1)} %moe_1.1) | data formatting | bytes 393216

commit v5 on v4

--- a/solution.py
+++ b/solution.py
@@ -20,13 +20,12 @@
 TOK_STEP = 16
 FF_CHUNK = 512
 LOOKAHEAD = 3
-OWN_FIRST = 5
+OWN_FIRST = 4
 PASS_CHUNK = 2048
 SHARED_CHUNK = 512
 SHARED_RING = 2
 Q_CHUNK = 512
 CHIP_CORES = 2
-ROW_TILE = 128
 
 
 def rms(vals):
@@ -42,7 +41,7 @@
 
 
 def attention_kernel(layer, capacity, q_heads, kv_heads, lens, x_ref, row_len_ref, ids_ref, wr_ref, wq, wk, wv, wo, kc, vc,
-                     a_ref, u_ref, meta_ref, wq_b, wk_b, wv_b, wo_b, k_b, v_b, q3, kn3, vn3, o3, attn, w_sem, q_sem, k_sem, v_sem):
+                     a_ref, u_ref, meta_ref, x_v, wr_v, wr_parts, wq_b, wk_b, wv_b, wo_b, k_b, v_b, q3, kn3, vn3, o3, attn, in_sem, w_sem, q_sem, k_sem, v_sem):
     n_tok, d_model = x_ref.shape
     rows = kc.shape[2]
     head_dim = kc.shape[3]
@@ -69,6 +68,10 @@
         for copy in cache_copies(step):
             copy.start()
 
+    x_copy = pltpu.make_async_copy(x_ref, x_v, in_sem.at[0])
+    wr_copy = pltpu.make_async_copy(wr_ref.at[layer], wr_v, in_sem.at[1])
+    x_copy.start()
+    wr_copy.start()
     k_copy.start()
     v_copy.start()
     q_copy(0).start()
@@ -76,13 +79,15 @@
     q3[:, q_heads:, :] = jnp.zeros((n_tok, q3.shape[1] - q_heads, head_dim), F32)
     kn3[:, q_heads:, :] = jnp.zeros((n_tok, q3.shape[1] - q_heads, head_dim), F32)
     vn3[:, q_heads:, :] = jnp.zeros((n_tok, q3.shape[1] - q_heads, head_dim), F32)
+    experts = wr_v.shape[0]
     all_tok = row_len_ref.shape[1]
     mine = lax.broadcasted_iota(jnp.int32, (n_tok, all_tok), 1) == first + lax.broadcasted_iota(jnp.int32, (n_tok, all_tok), 0)
 
     def column(row):
         return jnp.sum(jnp.where(mine, row.astype(F32), 0.0), axis=-1, keepdims=True)
 
-    x_f = x_ref[...].astype(F32)
+    x_copy.wait()
+    x_f = x_v[...].astype(F32)
     hidden = rms(x_f).astype(BF16)
     lane_d = lax.broadcasted_iota(jnp.int32, (n_tok, head_dim), 1)
     half = head_dim // 2
@@ -95,6 +100,14 @@
     def rotated(vals):
         return (vals * cosine + pltpu.roll(vals, half, 1) * sine).astype(BF16).astype(F32)
 
+    wr_copy.wait()
+    coarse = wr_v[...].astype(BF16)
+    rest = wr_v[...] - coarse.astype(F32)
+    middle = rest.astype(BF16)
+    fine = (rest - middle.astype(F32)).astype(BF16)
+    wr_parts[0:experts] = coarse.astype(F32)
+    wr_parts[experts:2 * experts] = middle.astype(F32)
+    wr_parts[2 * experts:3 * experts] = fine.astype(F32)
     k_copy.wait()
     q_copy(1).start()
     key = mm(hidden, wk_b[...])
@@ -155,15 +168,16 @@
     normed = rms(resid.astype(F32)).astype(BF16)
     u_ref[:, :d_model] = normed
 
-    logits = lax.dot_general(normed.astype(F32), wr_ref[layer], (((1,), (1,)), ((), ())), precision=lax.Precision.HIGHEST, preferred_element_type=F32)
-    experts = logits.shape[1]
+    logits = lax.dot_general(normed, wr_parts[...].astype(BF16), (((1,), (1,)), ((), ())), preferred_element_type=F32)
+    column_id = lax.broadcasted_iota(jnp.int32, logits.shape, 1)
+    column_id = lax.rem(column_id, experts).astype(F32)
     lane_e = lax.broadcasted_iota(jnp.int32, (n_tok, META), 1).astype(F32)
     id0 = column(ids_ref[layer, 0:1, :])
     id1 = column(ids_ref[layer, 1:2, :])
     pick0 = lane_e == id0
     pick1 = lane_e == id1
-    l0 = jnp.sum(jnp.where(pick0[:, :experts], logits, 0.0), axis=-1, keepdims=True)
-    l1 = jnp.sum(jnp.where(pick1[:, :experts], logits, 0.0), axis=-1, keepdims=True)
+    l0 = jnp.sum(jnp.where(column_id == id0, logits, 0.0), axis=-1, keepdims=True)
+    l1 = jnp.sum(jnp.where(column_id == id1, logits, 0.0), axis=-1, keepdims=True)
     peak = jnp.maximum(l0, l1)
     e0 = jnp.exp(l0 - peak)
     e1 = jnp.exp(l1 - peak)
@@ -177,13 +191,8 @@
     meta_ref[...] = jnp.where(lane_e == 0, slot0, jnp.where(lane_e == 1, slot1, jnp.where(lane_e == 2, e0 / total, e1 / total)))
 
 
-def row_blocks(capacity, blocks=((0, 2), (2, 4), (4, 8))):
-    sizes = [-(-(hi - lo) * capacity // ROW_TILE) * ROW_TILE if (hi - lo) * capacity < ROW_TILE else (hi - lo) * capacity for lo, hi in blocks]
-    return [sum(sizes[:i]) for i in range(len(sizes))], sizes
-
-
-def moe_kernel(layer, capacity, ep_size, u_ref, a_ref, meta_ref, sg, su, sd, wg, wu, wd, out_ref,
-               gath, back, picked, sent, acc_e, acc_s, pair, other_s, g_w, u_w, d_w, g_b, u_b, d_b, e_sem, s_sem, ag_send, ag_recv, ret_send, ret_recv, sum_send, sum_recv):
+def moe_kernel(layer, capacity, ep_size, u_hbm, a_hbm, meta_hbm, sg, su, sd, wg, wu, wd, out_ref,
+               u_ref, a_ref, meta_ref, gath, back, picked, sent, acc_e, acc_s, pair, other_s, g_w, u_w, d_w, g_b, u_b, d_b, e_sem, s_sem, ag_send, ag_recv, ret_send, ret_recv, sum_send, sum_recv, in_sem):
     n_tok = a_ref.shape[0]
     d_model = a_ref.shape[1]
     half = n_tok // 2
@@ -198,9 +207,6 @@
     p_left = lax.rem(partner + ep_size - 2, ep_size)
     p_far = lax.rem(partner + ep_size // 2, ep_size)
     places = [me, partner, far, p_far, right, p_right, left, p_left]
-    blocks = [(0, 2), (2, 4), (4, 8)]
-    starts, sizes = row_blocks(capacity, blocks)
-    row_of = {place: starts[i] + (place - lo) * capacity for i, (lo, hi) in enumerate(blocks) for place in range(lo, hi)}
 
     def expert_copies(chunk):
         cols = pl.ds(chunk * FF_CHUNK, FF_CHUNK)
@@ -214,14 +220,18 @@
         pairs = ((sg.at[layer, :, cols], g_b.at[slot]), (su.at[layer, :, cols], u_b.at[slot]), (sd.at[layer, cols], d_b.at[slot]))
         return [pltpu.make_async_copy(src, dst, s_sem.at[slot, i]) for i, (src, dst) in enumerate(pairs)]
 
+    in_copies = [pltpu.make_async_copy(src, dst, in_sem.at[i]) for i, (src, dst) in enumerate(((u_hbm, u_ref), (a_hbm, a_ref), (meta_hbm, meta_ref)))]
+    in_copies[0].start()
     for chunk in range(LOOKAHEAD):
         for copy in expert_copies(chunk):
             copy.start()
+    for copy in in_copies[1:]:
+        copy.start()
 
     barrier = pltpu.get_barrier_semaphore()
     for other in range(1, ep_size):
         pl.semaphore_signal(barrier, inc=1, device_id={"ep": lax.rem(me + other, ep_size)}, device_id_type=MESH)
-    gath[me] = u_ref[...]
+    in_copies[0].wait()
     pl.semaphore_wait(barrier, ep_size - 1)
 
     def piece(src, part):
@@ -249,14 +259,13 @@
 
     acc_s[...] = jnp.zeros_like(acc_s)
     acc_e[...] = jnp.zeros_like(acc_e)
-    picked[...] = jnp.zeros_like(picked)
     lane = lax.broadcasted_iota(jnp.int32, (n_tok, META), 1)
 
     def pick(src, codes, values, place):
         rank = jnp.sum(jnp.where(lane == me, codes.astype(F32), 0.0), axis=-1, keepdims=True)
         choose = jnp.where(lane.astype(F32) == rank, 1.0, 0.0).astype(BF16)
         rows = lax.dot_general(choose, values, (((0,), (0,)), ((), ())), preferred_element_type=F32)
-        picked[pl.ds(row_of[place], capacity)] = rows[:capacity].astype(BF16)
+        picked[pl.ds(place * capacity, capacity)] = rows[:capacity].astype(BF16)
 
     def pick_places(first, last):
         for place in range(first, last):
@@ -266,8 +275,8 @@
             else:
                 pick(src, gath[src, :, d_model:], gath[src, :, :d_model], place)
 
-    def expert_rows(block, chunk, width):
-        rows = pl.ds(starts[block], sizes[block])
+    def expert_rows(lo, hi, chunk, width):
+        rows = pl.ds(lo * capacity, (hi - lo) * capacity)
         cols = pl.ds(pl.multiple_of(chunk * width, width), width)
         x_rows = picked[rows]
         mid = (silu(mm(x_rows, g_w[:, cols])) * mm(x_rows, u_w[:, cols])).astype(BF16)
@@ -280,7 +289,7 @@
 
     def give_back(first, last):
         for place in range(first, last):
-            sent[place] = acc_e[pl.ds(row_of[place], capacity)].astype(BF16)
+            sent[place] = acc_e[pl.ds(place * capacity, capacity)].astype(BF16)
         for place in range(max(first, 1), last):
             return_copy(place).start()
 
@@ -293,7 +302,7 @@
             for copy in expert_copies(chunk + LOOKAHEAD):
                 copy.start()
 
-        expert_rows(0, chunk, FF_CHUNK)
+        expert_rows(0, 2, chunk, FF_CHUNK)
         return carry
 
     for part in (0, 1):
@@ -310,7 +319,8 @@
     for src, part in ((left, 1), (right, 0)):
         arrived(src, part)
         send(src, part, partner)
-    lax.fori_loop(4, OWN_FIRST, own_step, 0)
+    for copy in expert_copies(OWN_FIRST - 1 + LOOKAHEAD + 1) if OWN_FIRST + LOOKAHEAD < e_chunks else ():
+        copy.start()
     for slot in range(SHARED_RING):
         for copy in shared_copies(slot, slot):
             copy.start()
@@ -334,7 +344,7 @@
                 for copy in expert_copies(chunk):
                     copy.wait()
 
-        expert_rows(2, step, PASS_CHUNK)
+        expert_rows(4, 8, step, PASS_CHUNK)
 
         @pl.when(step == 0)
         def _():
@@ -352,17 +362,17 @@
     pick_places(2, 4)
 
     def far_step(step, carry):
-        expert_rows(1, step, PASS_CHUNK)
+        expert_rows(2, 4, step, PASS_CHUNK)
         return carry
 
     lax.fori_loop(0, e_chunks // per_step, far_step, 0)
     give_back(2, 4)
 
-    def own_rest(chunk, carry):
-        expert_rows(0, chunk, FF_CHUNK)
-        return carry
-
-    lax.fori_loop(OWN_FIRST, e_chunks, own_rest, 0)
+    def own_rest(step, carry):
+        expert_rows(0, 2, step, PASS_CHUNK)
+        return carry
+
+    lax.fori_loop(OWN_FIRST // per_step, e_chunks // per_step, own_rest, 0)
     give_back(0, 2)
     pair[pl.ds(0, n_tok)] = u_ref[:, :d_model]
     pair[pl.ds(n_tok, n_tok)] = gath[partner, :, :d_model]
@@ -395,6 +405,8 @@
         pltpu.make_async_remote_copy(src_ref=back.at[src], dst_ref=back.at[src], send_sem=ret_send.at[place], recv_sem=ret_recv.at[src],
                                      device_id={"ep": src}, device_id_type=MESH).wait_recv()
 
+    for copy in in_copies[1:]:
+        copy.wait()
     slot_lane = lax.broadcasted_iota(jnp.int32, (n_tok, ep_size * capacity), 1).astype(F32)
     table = back[...].reshape(ep_size * capacity, d_model)
     choose = jnp.concatenate([jnp.where(slot_lane == meta_ref[:, 0:1], 1.0, 0.0), jnp.where(slot_lane == meta_ref[:, 1:2], 1.0, 0.0)], axis=0).astype(BF16)
@@ -426,22 +438,23 @@
         k_rows = k_cache.reshape(n_layers, all_tok, rows, head_dim)
         v_rows = v_cache.reshape(n_layers, all_tok, rows, head_dim)
         ext = d_model + META
-        n_rows = sum(row_blocks(capacity)[1])
+        n_rows = ep_size * capacity
         x_cur = x_loc
         for layer in range(n_layers):
             resid, u_ext, meta = pl.pallas_call(
                 functools.partial(attention_kernel, layer, capacity, q_heads, kv_heads),
                 name=f"attention_{layer}",
                 out_shape=(jax.ShapeDtypeStruct((n_tok, d_model), BF16), jax.ShapeDtypeStruct((n_tok, ext), BF16), jax.ShapeDtypeStruct((n_tok, META), F32)),
-                in_specs=[SMEM] + [VMEM] * 4 + [ANY] * 6,
+                in_specs=[SMEM, ANY, VMEM, VMEM] + [ANY] * 7,
                 out_specs=(VMEM, VMEM, VMEM),
                 scratch_shapes=[
+                    pltpu.VMEM((n_tok, d_model), BF16), pltpu.VMEM(router_t.shape[1:], F32), pltpu.VMEM((3 * router_t.shape[1], d_model), F32),
                     pltpu.VMEM(w_query.shape[1:], BF16), pltpu.VMEM(w_key.shape[1:], BF16), pltpu.VMEM(w_value.shape[1:], BF16), pltpu.VMEM(w_out.shape[1:], BF16),
                     pltpu.VMEM((n_tok, rows, head_dim), BF16), pltpu.VMEM((n_tok, rows, head_dim), BF16),
                     pltpu.VMEM((n_tok, pad_heads, head_dim), F32), pltpu.VMEM((n_tok, pad_heads, head_dim), F32),
                     pltpu.VMEM((n_tok, pad_heads, head_dim), F32), pltpu.VMEM((n_tok, pad_heads, head_dim), F32),
                     pltpu.VMEM((n_tok, q_heads * head_dim), BF16),
-                    pltpu.SemaphoreType.DMA((3,)), pltpu.SemaphoreType.DMA((q_heads * head_dim // Q_CHUNK,)), pltpu.SemaphoreType.DMA((n_tok // TOK_STEP,)), pltpu.SemaphoreType.DMA((n_tok // TOK_STEP,)),
+                    pltpu.SemaphoreType.DMA((2,)), pltpu.SemaphoreType.DMA((3,)), pltpu.SemaphoreType.DMA((q_heads * head_dim // Q_CHUNK,)), pltpu.SemaphoreType.DMA((n_tok // TOK_STEP,)), pltpu.SemaphoreType.DMA((n_tok // TOK_STEP,)),
                 ],
                 compiler_params=pltpu.CompilerParams(vmem_limit_bytes=VMEM_BYTES),
             )(cache_len, x_cur, row_len, ids_t, router_t, w_query, w_key, w_value, w_out, k_rows, v_rows)
@@ -449,9 +462,10 @@
                 functools.partial(moe_kernel, layer, capacity, ep_size),
                 name=f"moe_{layer}",
                 out_shape=jax.ShapeDtypeStruct((n_tok, d_model), BF16),
-                in_specs=[VMEM] * 3 + [ANY] * 6,
+                in_specs=[ANY] * 9,
                 out_specs=VMEM,
                 scratch_shapes=[
+                    pltpu.VMEM((n_tok, ext), BF16), pltpu.VMEM((n_tok, d_model), BF16), pltpu.VMEM((n_tok, META), F32),
                     pltpu.VMEM((ep_size, n_tok, ext), BF16), pltpu.VMEM((ep_size, capacity, d_model), BF16),
                     pltpu.VMEM((n_rows, d_model), BF16), pltpu.VMEM((ep_size, capacity, d_model), BF16),
                     pltpu.VMEM((n_rows, d_model), F32), pltpu.VMEM((CHIP_CORES * n_tok, d_model), F32),
@@ -459,7 +473,7 @@
                     pltpu.VMEM(w_gate.shape[2:], BF16), pltpu.VMEM(w_up.shape[2:], BF16), pltpu.VMEM(w_down.shape[2:], BF16),
                     pltpu.VMEM((SHARED_RING, d_model, SHARED_CHUNK), BF16), pltpu.VMEM((SHARED_RING, d_model, SHARED_CHUNK), BF16), pltpu.VMEM((SHARED_RING, SHARED_CHUNK, d_model), BF16),
                     pltpu.SemaphoreType.DMA((w_gate.shape[3] // FF_CHUNK, 3)), pltpu.SemaphoreType.DMA((SHARED_RING, 3)), pltpu.SemaphoreType.DMA((14,)), pltpu.SemaphoreType.DMA((ep_size, 2)),
-                    pltpu.SemaphoreType.DMA((ep_size,)), pltpu.SemaphoreType.DMA((ep_size,)), pltpu.SemaphoreType.DMA, pltpu.SemaphoreType.DMA,
+                    pltpu.SemaphoreType.DMA((ep_size,)), pltpu.SemaphoreType.DMA((ep_size,)), pltpu.SemaphoreType.DMA, pltpu.SemaphoreType.DMA, pltpu.SemaphoreType.DMA((3,)),
                 ],
                 compiler_params=pltpu.CompilerParams(vmem_limit_bytes=VMEM_BYTES, collective_id=layer, has_side_effects=True),
             )(u_ext, resid, meta, shared_gate, shared_up, shared_down, w_gate, w_up, w_down)

time: 104 us -> 105 us (level)
    pallas_call x2, Pallas kernels: 77 us -> 80.2 us  [body(): pl.pallas_call(functools.partial(moe_kernel, layer, capacity, ep_size), n...]
    pallas_call x2, Pallas kernels: 24.8 us -> 23 us  [body(): pl.pallas_call(functools.partial(attention_kernel, layer, capacity, q_hea...]
where the time goes in v5:
time: 105 us
  Pallas kernels  103 us (98%)
  local copies, waits for them, and re-layouts  1.62 us (2%)
    pallas_call x2, Pallas kernels, body(): pl.pallas_call(functools.partial(moe_kernel, layer, capacity, ep_size), n...  80.2 us
    pallas_call x2, Pallas kernels, body(): pl.pallas_call(functools.partial(attention_kernel, layer, capacity, q_hea...  23 us

profile of v5, /device:TPU:97, one launch (start us, length us, event | category | flops | bytes accessed | tf_op | source)
XLA Modules:
  0.0 104.9 jit_solution(3931553343740507452)
XLA Ops:
  0.0 11.5 %attention_0.1 = (bf16[64,1536]{1,0:T(8,128)(2,1)}, bf16[64,1664]{1,0:T(8,128)(2,1)}, f32[64,128]{1,0:T(8,128)}) custom-call(s32[256]{0:T(256)} %lens.3, bf16[64,1536]{1,0:T(8,128)(2,1)} %x_ref.1, s32[1,256]{1,0:T(1,128)} %bitcast.13, s32[2,2,256]{2,1,0:T(2,128)} %bitcast.11, f32[2,8,1536]{2,1,0:T(8,128)} %bitcast.9, bf16[2,1536,1536]{2,1,0:T(8,128)(2,1)} %wq.3, ...), custom_call_target="tpu_custom_call" | custom-call | tf_op jit(solution)/shard_map/attention_0/pallas_call | solution.py:444
  11.5 41.8 %moe_0.1.x_ref = bf16[64,1536]{1,0:T(8,128)(2,1)} custom-call(bf16[64,1664]{1,0:T(8,128)(2,1)} %get-tuple-element.11.u_hbm, bf16[64,1536]{1,0:T(8,128)(2,1)} %get-tuple-element.12.a_hbm, f32[64,128]{1,0:T(8,128)} %get-tuple-element.13.meta_hbm, bf16[2,1536,4096]{2,1,0:T(8,128)(2,1)} %sg.3, bf16[2,1536,4096]{2,1,0:T(8,128)(2,1)} %su.3, ...), custom_call_target="tpu_custom_call" | custom-call | tf_op jit(solution)/shard_map/moe_0/pallas_call | solution.py:461
  53.4 11.5 %attention_1.1 = (bf16[64,1536]{1,0:T(8,128)(2,1)}, bf16[64,1664]{1,0:T(8,128)(2,1)}, f32[64,128]{1,0:T(8,128)}) custom-call(s32[256]{0:T(256)} %lens.3, bf16[64,1536]{1,0:T(8,128)(2,1)} %moe_0.1.x_ref, s32[1,256]{1,0:T(1,128)} %bitcast.14, s32[2,2,256]{2,1,0:T(2,128)} %bitcast.12, f32[2,8,1536]{2,1,0:T(8,128)} %bitcast.10, bf16[2,1536,1536]{2,1,0:T(8,128)(2,1)} %wq.3, ...), custom_call_target="tpu_custom_call" | custom-call | tf_op jit(solution)/shard_map/attention_1/pallas_call | solution.py:444
  64.9 38.4 %moe_1.1 = bf16[64,1536]{1,0:T(8,128)(2,1)} custom-call(bf16[64,1664]{1,0:T(8,128)(2,1)} %get-tuple-element.14.u_hbm, bf16[64,1536]{1,0:T(8,128)(2,1)} %get-tuple-element.15.a_hbm, f32[64,128]{1,0:T(8,128)} %get-tuple-element.16.meta_hbm, bf16[2,1536,4096]{2,1,0:T(8,128)(2,1)} %sg.3, bf16[2,1536,4096]{2,1,0:T(8,128)(2,1)} %su.3, bf16[2,4096,1536]{2,1,0:T(8,128)(2,1)} %sd.3, ...), custom_call_target="tpu_custom_call" | custom-call | tf_op jit(solution)/shard_map/moe_1/pallas_call | solution.py:461
  103.3 1.6 %copy.18 = bf16[64,1536]{1,0:T(8,128)(2,1)} copy(bf16[64,1536]{1,0:T(8,128)(2,1)} %moe_1.1) | data formatting | bytes 393216

commit v6 on v4

--- a/solution.py
+++ b/solution.py
@@ -42,7 +42,7 @@
 
 
 def attention_kernel(layer, capacity, q_heads, kv_heads, lens, x_ref, row_len_ref, ids_ref, wr_ref, wq, wk, wv, wo, kc, vc,
-                     a_ref, u_ref, meta_ref, wq_b, wk_b, wv_b, wo_b, k_b, v_b, q3, kn3, vn3, o3, attn, w_sem, q_sem, k_sem, v_sem):
+                     a_ref, u_ref, meta_ref, x_v, wr_v, wr_parts, wq_b, wk_b, wv_b, wo_b, k_b, v_b, q3, kn3, vn3, o3, attn, in_sem, w_sem, q_sem, k_sem, v_sem):
     n_tok, d_model = x_ref.shape
     rows = kc.shape[2]
     head_dim = kc.shape[3]
@@ -69,6 +69,10 @@
         for copy in cache_copies(step):
             copy.start()
 
+    x_copy = pltpu.make_async_copy(x_ref, x_v, in_sem.at[0])
+    wr_copy = pltpu.make_async_copy(wr_ref.at[layer], wr_v, in_sem.at[1])
+    x_copy.start()
+    wr_copy.start()
     k_copy.start()
     v_copy.start()
     q_copy(0).start()
@@ -76,13 +80,15 @@
     q3[:, q_heads:, :] = jnp.zeros((n_tok, q3.shape[1] - q_heads, head_dim), F32)
     kn3[:, q_heads:, :] = jnp.zeros((n_tok, q3.shape[1] - q_heads, head_dim), F32)
     vn3[:, q_heads:, :] = jnp.zeros((n_tok, q3.shape[1] - q_heads, head_dim), F32)
+    experts = wr_v.shape[0]
     all_tok = row_len_ref.shape[1]
     mine = lax.broadcasted_iota(jnp.int32, (n_tok, all_tok), 1) == first + lax.broadcasted_iota(jnp.int32, (n_tok, all_tok), 0)
 
     def column(row):
         return jnp.sum(jnp.where(mine, row.astype(F32), 0.0), axis=-1, keepdims=True)
 
-    x_f = x_ref[...].astype(F32)
+    x_copy.wait()
+    x_f = x_v[...].astype(F32)
     hidden = rms(x_f).astype(BF16)
     lane_d = lax.broadcasted_iota(jnp.int32, (n_tok, head_dim), 1)
     half = head_dim // 2
@@ -95,6 +101,14 @@
     def rotated(vals):
         return (vals * cosine + pltpu.roll(vals, half, 1) * sine).astype(BF16).astype(F32)
 
+    wr_copy.wait()
+    coarse = wr_v[...].astype(BF16)
+    rest = wr_v[...] - coarse.astype(F32)
+    middle = rest.astype(BF16)
+    fine = (rest - middle.astype(F32)).astype(BF16)
+    wr_parts[0:experts] = coarse.astype(F32)
+    wr_parts[experts:2 * experts] = middle.astype(F32)
+    wr_parts[2 * experts:3 * experts] = fine.astype(F32)
     k_copy.wait()
     q_copy(1).start()
     key = mm(hidden, wk_b[...])
@@ -155,15 +169,16 @@
     normed = rms(resid.astype(F32)).astype(BF16)
     u_ref[:, :d_model] = normed
 
-    logits = lax.dot_general(normed.astype(F32), wr_ref[layer], (((1,), (1,)), ((), ())), precision=lax.Precision.HIGHEST, preferred_element_type=F32)
-    experts = logits.shape[1]
+    logits = lax.dot_general(normed, wr_parts[...].astype(BF16), (((1,), (1,)), ((), ())), preferred_element_type=F32)
+    column_id = lax.broadcasted_iota(jnp.int32, logits.shape, 1)
+    column_id = lax.rem(column_id, experts).astype(F32)
     lane_e = lax.broadcasted_iota(jnp.int32, (n_tok, META), 1).astype(F32)
     id0 = column(ids_ref[layer, 0:1, :])
     id1 = column(ids_ref[layer, 1:2, :])
     pick0 = lane_e == id0
     pick1 = lane_e == id1
-    l0 = jnp.sum(jnp.where(pick0[:, :experts], logits, 0.0), axis=-1, keepdims=True)
-    l1 = jnp.sum(jnp.where(pick1[:, :experts], logits, 0.0), axis=-1, keepdims=True)
+    l0 = jnp.sum(jnp.where(column_id == id0, logits, 0.0), axis=-1, keepdims=True)
+    l1 = jnp.sum(jnp.where(column_id == id1, logits, 0.0), axis=-1, keepdims=True)
     peak = jnp.maximum(l0, l1)
     e0 = jnp.exp(l0 - peak)
     e1 = jnp.exp(l1 - peak)
@@ -433,15 +448,16 @@
                 functools.partial(attention_kernel, layer, capacity, q_heads, kv_heads),
                 name=f"attention_{layer}",
                 out_shape=(jax.ShapeDtypeStruct((n_tok, d_model), BF16), jax.ShapeDtypeStruct((n_tok, ext), BF16), jax.ShapeDtypeStruct((n_tok, META), F32)),
-                in_specs=[SMEM] + [VMEM] * 4 + [ANY] * 6,
+                in_specs=[SMEM, ANY, VMEM, VMEM] + [ANY] * 7,
                 out_specs=(VMEM, VMEM, VMEM),
                 scratch_shapes=[
+                    pltpu.VMEM((n_tok, d_model), BF16), pltpu.VMEM(router_t.shape[1:], F32), pltpu.VMEM((3 * router_t.shape[1], d_model), F32),
                     pltpu.VMEM(w_query.shape[1:], BF16), pltpu.VMEM(w_key.shape[1:], BF16), pltpu.VMEM(w_value.shape[1:], BF16), pltpu.VMEM(w_out.shape[1:], BF16),
                     pltpu.VMEM((n_tok, rows, head_dim), BF16), pltpu.VMEM((n_tok, rows, head_dim), BF16),
                     pltpu.VMEM((n_tok, pad_heads, head_dim), F32), pltpu.VMEM((n_tok, pad_heads, head_dim), F32),
                     pltpu.VMEM((n_tok, pad_heads, head_dim), F32), pltpu.VMEM((n_tok, pad_heads, head_dim), F32),
                     pltpu.VMEM((n_tok, q_heads * head_dim), BF16),
-                    pltpu.SemaphoreType.DMA((3,)), pltpu.SemaphoreType.DMA((q_heads * head_dim // Q_CHUNK,)), pltpu.SemaphoreType.DMA((n_tok // TOK_STEP,)), pltpu.SemaphoreType.DMA((n_tok // TOK_STEP,)),
+                    pltpu.SemaphoreType.DMA((2,)), pltpu.SemaphoreType.DMA((3,)), pltpu.SemaphoreType.DMA((q_heads * head_dim // Q_CHUNK,)), pltpu.SemaphoreType.DMA((n_tok // TOK_STEP,)), pltpu.SemaphoreType.DMA((n_tok // TOK_STEP,)),
                 ],
                 compiler_params=pltpu.CompilerParams(vmem_limit_bytes=VMEM_BYTES),
             )(cache_len, x_cur, row_len, ids_t, router_t, w_query, w_key, w_value, w_out, k_rows, v_rows)

time: 104 us -> 102 us (0.981)
  Pallas kernels: 102 us -> 100 us
    pallas_call x2, Pallas kernels: 24.8 us -> 23 us  [body(): pl.pallas_call(functools.partial(attention_kernel, layer, capacity, q_hea...]
where the time goes in v6:
time: 102 us
  Pallas kernels  100 us (98%)
  local copies, waits for them, and re-layouts  1.62 us (2%)
    pallas_call x2, Pallas kernels, body(): pl.pallas_call(functools.partial(moe_kernel, layer, capacity, ep_size), n...  77 us
    pallas_call x2, Pallas kernels, body(): pl.pallas_call(functools.partial(attention_kernel, layer, capacity, q_hea...  23 us

profile of v6, /device:TPU:97, one launch (start us, length us, event | category | flops | bytes accessed | tf_op | source)
XLA Modules:
  0.0 101.7 jit_solution(14848848693298810950)
XLA Ops:
  0.0 11.5 %attention_0.1 = (bf16[64,1536]{1,0:T(8,128)(2,1)}, bf16[64,1664]{1,0:T(8,128)(2,1)}, f32[64,128]{1,0:T(8,128)}) custom-call(s32[256]{0:T(256)} %lens.3, bf16[64,1536]{1,0:T(8,128)(2,1)} %x_ref.1, s32[1,256]{1,0:T(1,128)} %bitcast.13, s32[2,2,256]{2,1,0:T(2,128)} %bitcast.11, f32[2,8,1536]{2,1,0:T(8,128)} %bitcast.9, bf16[2,1536,1536]{2,1,0:T(8,128)(2,1)} %wq.3, ...), custom_call_target="tpu_custom_call" | custom-call | tf_op jit(solution)/shard_map/attention_0/pallas_call | solution.py:447
  11.5 39.6 %moe_0.1.x_ref = bf16[64,1536]{1,0:T(8,128)(2,1)} custom-call(bf16[64,1664]{1,0:T(8,128)(2,1)} %get-tuple-element.11.u_ref, bf16[64,1536]{1,0:T(8,128)(2,1)} %get-tuple-element.12.a_ref, f32[64,128]{1,0:T(8,128)} %get-tuple-element.13.meta_ref, bf16[2,1536,4096]{2,1,0:T(8,128)(2,1)} %sg.3, bf16[2,1536,4096]{2,1,0:T(8,128)(2,1)} %su.3, ...), custom_call_target="tpu_custom_call" | custom-call | tf_op jit(solution)/shard_map/moe_0/pallas_call | solution.py:464
  51.1 11.5 %attention_1.1 = (bf16[64,1536]{1,0:T(8,128)(2,1)}, bf16[64,1664]{1,0:T(8,128)(2,1)}, f32[64,128]{1,0:T(8,128)}) custom-call(s32[256]{0:T(256)} %lens.3, bf16[64,1536]{1,0:T(8,128)(2,1)} %moe_0.1.x_ref, s32[1,256]{1,0:T(1,128)} %bitcast.14, s32[2,2,256]{2,1,0:T(2,128)} %bitcast.12, f32[2,8,1536]{2,1,0:T(8,128)} %bitcast.10, bf16[2,1536,1536]{2,1,0:T(8,128)(2,1)} %wq.3, ...), custom_call_target="tpu_custom_call" | custom-call | tf_op jit(solution)/shard_map/attention_1/pallas_call | solution.py:447
  62.6 37.4 %moe_1.1 = bf16[64,1536]{1,0:T(8,128)(2,1)} custom-call(bf16[64,1664]{1,0:T(8,128)(2,1)} %get-tuple-element.14.u_ref, bf16[64,1536]{1,0:T(8,128)(2,1)} %get-tuple-element.15.a_ref, f32[64,128]{1,0:T(8,128)} %get-tuple-element.16.meta_ref, bf16[2,1536,4096]{2,1,0:T(8,128)(2,1)} %sg.3, bf16[2,1536,4096]{2,1,0:T(8,128)(2,1)} %su.3, bf16[2,4096,1536]{2,1,0:T(8,128)(2,1)} %sd.3, ...), custom_call_target="tpu_custom_call" | custom-call | tf_op jit(solution)/shard_map/moe_1/pallas_call | solution.py:464
  100.1 1.6 %copy.18 = bf16[64,1536]{1,0:T(8,128)(2,1)} copy(bf16[64,1536]{1,0:T(8,128)(2,1)} %moe_1.1) | data formatting | bytes 393216
